TPU v7x, 256 devices: a whole 4x4x8 slice. The times are simulated.
256 devices in a mesh: feat: 64 (over z, y, x_hi), row: 2 (over x_lo), col: 2 (over core).
Axes of the slice: x: 4 (x_hi: 2, x_lo: 2; x = x_hi * 2 + x_lo), y: 4, z: 8, core: 2. Of those that a mesh axis runs over, the one named last changes fastest.
Arguments:
- local_x: float32 [4, 256, 256], P(('row', 'col'), 'feat'), may hold values from -4 to 4
- dual_var: float32 [4, 256, 256], P(('row', 'col'), 'feat'), may hold values from -2 to 2
- consensus_old: float32 [256, 256], P('feat'), may hold values from -4 to 4
- blocks_data: bfloat16 [4, 256, 512, 256], P(('row', 'col'), 'feat'), may hold values from -0.375 to 0.375
- row_index: int32 [4, 256, 512], P(('row', 'col'), 'feat'), may hold values from 0 to 16383, as said below
- labels: int32 [4, 16384], P(('row', 'col')), may hold values 0 or 1
Outputs:
- solved_x: float32 [4, 256, 256], P(('row', 'col'), 'feat')
- dual_new: float32 [4, 256, 256], P(('row', 'col'), 'feat')
- consensus: float32 [256, 256], P('feat')
- norms: float32 [2], replicated
Inputs may be any that keep to these rules, and one draw needn't show every extreme that they name: `row_index`: the 512 rows of one block are distinct samples of its shard; a sample may appear in no block or in several.
All inputs are finite; a program needn't handle non-finite values. No bound on the sum of `labels` on one device may be relied on, other than what follows from the above.
Results may differ from a plain program's by a relative error of at most 0.0019.
Values sent between devices are 32-bit elements; how exact they have to be, the bound alone decides.
No kernel may reach another device: no remote copies, remote signals or barrier semaphores. Data moves between devices by JAX's collectives and lax.ppermute only.
A program may use at most 64 MiB of HBM per device.

v0:
```python
import jax
import jax.numpy as jnp
from jax import lax
from jax.sharding import Mesh
from jax.sharding import PartitionSpec as P

NEWTON_STEPS = 2
CG_STEPS = 3
FEAT = ("feat_0", "feat_1", "feat_2")
FEAT_ROW_COL = ("feat_0", "feat_1", "feat_2", "row", "col")


penalty = 1.0
damping = 0.5
threshold = 0.05


def filled_up(lines, size):
    spare = -len(lines) % size
    return jnp.pad(lines, [(0, spare)] + [(0, 0)] * (lines.ndim - 1))


def copy_for_each(x, axis):
    copies = jnp.broadcast_to(x, (lax.axis_size(axis), *x.shape))
    return lax.all_to_all(copies, axis, split_axis=0, concat_axis=0, tiled=True)


def joined_along(parts, dim):
    parts = jnp.moveaxis(parts, 0, dim)
    dims = parts.shape
    return parts.reshape(*dims[:dim], dims[dim] * dims[dim + 1], *dims[dim + 2 :])


def gather_directly(x, axis, dim):
    parts = copy_for_each(x, axis)
    return joined_along(parts, dim)


def cut_along(x, dim, size):
    before, after = (x.shape[:dim], x.shape[dim + 1 :])
    return jnp.moveaxis(x.reshape(*before, size, -1, *after), dim, 0)


def summed_on_arrival(x, axis, dim):
    size = lax.axis_size(axis)
    parts = lax.all_to_all(cut_along(x, dim, size), axis, 0, 0, tiled=True)
    return jnp.sum(parts, axis=0)


def total_of(x, axes):
    lines = x.reshape(-1)
    padded = filled_up(lines, lax.axis_size(axes))
    whole = gather_directly(summed_on_arrival(padded, axes, 0), axes, 0)
    return lax.slice_in_dim(whole, 0, len(lines)).reshape(x.shape)


def of_everyone(x, axis):
    everything = copy_for_each(x, axis)
    return jnp.sum(everything, axis=0)


def by_axis(x, axes):
    for axis in axes:
        x = lax.psum(x, axis)
    return x


def shrink(values):
    return jnp.sign(values) * jnp.maximum(jnp.abs(values) - threshold, 0.0)


def conjugate_solve(hessian, gradient):
    delta = jnp.zeros_like(gradient)
    residual = gradient
    direction = gradient
    power = jnp.sum(residual * residual, axis=1)
    for cg_step in range(CG_STEPS):
        image = jnp.einsum("bkl,bl->bk", hessian, direction, precision=lax.Precision.HIGHEST)
        alpha = power / jnp.sum(direction * image, axis=1)
        delta = delta + alpha[:, None] * direction
        residual = residual - alpha[:, None] * image
        power_next = jnp.sum(residual * residual, axis=1)
        direction = residual + (power_next / power)[:, None] * direction
        power = power_next
    return delta


def local(local_x, dual_var, consensus_old, blocks_data, row_index, labels):
    iterate = local_x[0]
    dual_local = dual_var[0]
    block_rows = blocks_data[0]
    index_rows = row_index[0]
    targets = labels[0].astype(jnp.float32)
    samples = targets.shape[0]
    target = consensus_old - dual_local
    flat_index = index_rows.reshape(-1)
    identity = jnp.eye(iterate.shape[1], dtype=jnp.float32)
    for newton_step in range(NEWTON_STEPS):
        rounded = iterate.astype(jnp.bfloat16)
        partial_value = jnp.einsum(
            "brk,bk->br", block_rows, rounded, preferred_element_type=jnp.float32
        )
        local_margins = jax.ops.segment_sum(
            partial_value.reshape(-1), flat_index, num_segments=samples
        )
        margins = total_of(local_margins, FEAT)
        prob = jax.nn.sigmoid(margins)
        misfit = prob - targets
        weights = prob * (1.0 - prob)
        misfit_rows = misfit[index_rows].astype(jnp.bfloat16)
        gradient = jnp.einsum(
            "brk,br->bk", block_rows, misfit_rows, preferred_element_type=jnp.float32
        )
        gradient = gradient + penalty * (iterate - target)
        weighted = (block_rows * weights[index_rows][:, :, None]).astype(jnp.bfloat16)
        hessian = (
            jnp.einsum("brk,brl->bkl", block_rows, weighted, preferred_element_type=jnp.float32)
            + penalty * identity
        )
        delta = conjugate_solve(hessian, gradient)
        iterate = iterate - damping * delta
    shards = lax.axis_size(("row", "col"))
    combined = iterate + dual_local
    totals = of_everyone(combined, ("row", "col"))
    consensus = shrink(totals / jnp.float32(shards))
    dual_next = dual_local + iterate - consensus
    primal_local = jnp.sum((iterate - consensus) ** 2)
    change_local = jnp.sum((consensus - consensus_old) ** 2)
    primal_total, change_total = (
        by_axis(primal_local, FEAT_ROW_COL),
        by_axis(change_local / jnp.float32(shards), FEAT_ROW_COL),
    )
    norms = jnp.stack(
        [jnp.sqrt(primal_total), penalty * jnp.sqrt(jnp.float32(shards) * change_total)]
    )
    return (iterate[None], dual_next[None], consensus, norms)


def solution(mesh):
    torus = Mesh(
        mesh.devices.reshape(8, 4, 2, mesh.shape["row"], mesh.shape["col"]),
        ("feat_0", "feat_1", "feat_2", "row", "col"),
    )
    placed = (
        P(("row", "col"), FEAT, None),
        P(("row", "col"), FEAT, None),
        P(FEAT, None),
        P(("row", "col"), FEAT, None, None),
        P(("row", "col"), FEAT, None),
        P(("row", "col"), None),
    )
    return jax.shard_map(
        local,
        mesh=torus,
        in_specs=placed,
        out_specs=(
            P(("row", "col"), FEAT, None),
            P(("row", "col"), FEAT, None),
            P(FEAT, None),
            P(),
        ),
        check_vma=False,
    )
```

profile of v0, /device:TPU:1, one launch (start us, length us, event | category | flops | bytes accessed | tf_op | source)
XLA Modules:
  0.0 213.6 jit_solution(8987383086924766513)
XLA Ops:
  0.7 0.7 fusion.68
  1.4 1.6 fusion.26
  3.0 11.8 %scatter_custom_fusion = f32[16384]{0:T(1024)} fusion(s32[2048]{0:T(1024)S(1)} %bitcast.161, f32[2048]{0:T(1024)S(1)} %bitcast.163, f32[]{:T(128)} %constant.9.clone.1), kind=kCustom, calls=%fused_computation.44 | custom fusion | flops 2048 | bytes 65540 | tf_op jit(solution)/shard_map/scatter-add | solution.py:103
  14.8 15.1 %all-to-all-start = ((f32[64,1,256]{2,1,0:T(1,128)}), f32[64,1,256]{2,1,0:T(1,128)S(1)}, u32[]{:S(2)}, u32[]{:S(2)}) async-start(f32[64,1,256]{2,1,0:T(1,128)} %bitcast.4), calls=%async_computation | async-start | bytes 131072 | tf_op jit(solution)/shard_map/all_to_all | solution.py:46
  30.0 11.0 %all-to-all-done = f32[64,1,256]{2,1,0:T(1,128)S(1)} async-done(((f32[64,1,256]{2,1,0:T(1,128)}), f32[64,1,256]{2,1,0:T(1,128)S(1)}, u32[]{:S(2)}, u32[]{:S(2)}) %all-to-all-start) | async-done | bytes 65568 | tf_op jit(solution)/shard_map/all_to_all | solution.py:46
  41.0 0.1 reduce_sum.153
  41.1 0.7 broadcast_in_dim.10
  41.8 4.6 %all-to-all-start.1 = ((f32[64,1,256]{2,1,0:T(1,128)}), f32[64,1,256]{2,1,0:T(1,128)S(1)}, u32[]{:S(2)}, u32[]{:S(2)}) async-start(f32[64,1,256]{2,1,0:T(1,128)} %broadcast_in_dim.10), calls=%async_computation.1 | async-start | bytes 131072 | tf_op jit(solution)/shard_map/all_to_all | solution.py:25
  46.5 10.9 %all-to-all-done.1 = f32[64,1,256]{2,1,0:T(1,128)S(1)} async-done(((f32[64,1,256]{2,1,0:T(1,128)}), f32[64,1,256]{2,1,0:T(1,128)S(1)}, u32[]{:S(2)}, u32[]{:S(2)}) %all-to-all-start.1) | async-done | bytes 65568 | tf_op jit(solution)/shard_map/all_to_all | solution.py:25
  57.5 11.8 %gather_fusion.1 = f32[2048]{0:T(1024)S(1)} fusion(f32[16384]{0:T(1024)S(1)} %subtract_multiply_fusion.1, s32[2048]{0:T(1024)S(1)} %broadcast_clamp_fusion), kind=kCustom, calls=%fused_computation.1 | custom fusion | bytes 24576 | tf_op jit(solution)/shard_map/gather | solution.py:115
  69.3 13.1 %gather_fusion = bf16[2048]{0:T(1024)(128)(2,1)S(1)} fusion(bf16[16384]{0:T(1024)(128)(2,1)S(1)} %sub.52, s32[2048]{0:T(1024)S(1)} %broadcast_clamp_fusion), kind=kCustom, calls=%fused_computation | custom fusion | bytes 16384 | tf_op jit(solution)/shard_map/gather | solution.py:110
  82.4 0.2 fusion.24
  82.7 0.9 fusion.9
  83.6 0.7 fusion.65
  84.3 0.1 fusion.52
  84.5 0.2 multiply_reduce_fusion.6
  84.7 0.7 fusion.63
  85.4 0.1 fusion.50
  85.5 0.2 multiply_reduce_fusion.5
  85.8 0.7 fusion.61
  86.5 0.1 fusion.49
  86.6 0.1 convert_bitcast_fusion
  86.7 0.4 fusion.20
  87.1 11.3 %scatter_custom_fusion.1 = f32[16384]{0:T(1024)S(1)} fusion(s32[2048]{0:T(1024)S(1)} %bitcast.162, f32[2048]{0:T(1024)S(1)} %bitcast.164, f32[]{:T(128)} %constant.9.clone.1), kind=kCustom, calls=%fused_computation.42 | custom fusion | flops 2048 | bytes 65540 | tf_op jit(solution)/shard_map/scatter-add | solution.py:103
  98.4 14.8 %all_to_all.35 = f32[64,1,256]{2,1,0:T(1,128)S(1)} all-to-all(f32[64,1,256]{2,1,0:T(1,128)S(1)} %bitcast.149), channel_id=1, replica_groups=mesh['feat_0'=8,'feat_1'=4,'feat_2'=2,'row'=2,'col'=2] {'feat_0','feat_1..., dimensions={0} | all-to-all | bytes 131072 | tf_op jit(solution)/shard_map/all_to_all | solution.py:46
  113.2 0.1 reduce_sum.160
  113.3 14.8 %all_to_all.36 = f32[64,1,256]{2,1,0:T(1,128)S(1)} all-to-all(f32[64,1,256]{2,1,0:T(1,128)S(1)} %broadcast_in_dim.11), channel_id=1, replica_groups=mesh['feat_0'=8,'feat_1'=4,'feat_2'=2,'row'=2,'col'=2] {'feat_0','feat_1..., dimensions={0} | all-to-all | bytes 131072 | tf_op jit(solution)/shard_map/all_to_all | solution.py:25
  128.2 13.1 %gather_fusion.2 = bf16[2048]{0:T(1024)(128)(2,1)S(1)} fusion(bf16[16384]{0:T(1024)(128)(2,1)S(1)} %sub.59, s32[2048]{0:T(1024)S(1)} %broadcast_clamp_fusion), kind=kCustom, calls=%fused_computation.2 | custom fusion | bytes 16384 | tf_op jit(solution)/shard_map/gather | solution.py:110
  141.3 11.8 %gather_fusion.3 = f32[2048]{0:T(1024)S(1)} fusion(f32[16384]{0:T(1024)S(1)} %subtract_multiply_fusion, s32[2048]{0:T(1024)S(1)} %broadcast_clamp_fusion), kind=kCustom, calls=%fused_computation.3 | custom fusion | bytes 24576 | tf_op jit(solution)/shard_map/gather | solution.py:115
  153.1 0.2 fusion.18
  153.3 0.9 fusion.15
  154.3 0.7 fusion.58
  155.0 0.1 fusion.47
  155.1 0.2 multiply_reduce_fusion.3
  155.4 0.7 fusion.56
  156.1 0.1 fusion.45
  156.2 0.2 multiply_reduce_fusion.2
  156.5 0.7 fusion.54
  157.1 0.1 fusion.44
  157.3 11.1 %all_to_all.37 = f32[4,4,256]{2,1,0:T(4,128)S(1)} all-to-all(f32[4,4,256]{2,1,0:T(4,128)S(1)} %broadcast_in_dim.13), channel_id=1, replica_groups=mesh['feat_0'=8,'feat_1'=4,'feat_2'=2,'row'=2,'col'=2] {'row','col'}, dimensions={0} | all-to-all | bytes 32768 | tf_op jit(solution)/shard_map/all_to_all | solution.py:25
  168.5 0.7 multiply_reduce_fusion.1
  169.2 0.6 subtract_bitcast_fusion
  170.5 11.9 %all-reduce = (f32[]{:T(128)}, f32[]{:T(128)}) all-reduce(f32[]{:T(128)S(6)} %div.107, f32[]{:T(128)} %get-tuple-element.4), channel_id=1, replica_groups=mesh['feat_0'=8,'feat_1'=4,'feat_2'=2,'row'=2,'col'=2] {'feat_0'}, use_global_device_ids=true, to_apply=%region_24.25 | all-reduce | flops 2 | bytes 16 | tf_op jit(solution)/shard_map/psum | solution.py:64
  182.4 7.4 %all-reduce.1 = (f32[]{:T(128)}, f32[]{:T(128)}) all-reduce(f32[]{:T(128)} %get-tuple-element.10, f32[]{:T(128)} %get-tuple-element.11), channel_id=1, replica_groups=mesh['feat_0'=8,'feat_1'=4,'feat_2'=2,'row'=2,'col'=2] {'feat_1'}, use_global_device_ids=true, to_apply=%region_25.26 | all-reduce | flops 2 | bytes 16 | tf_op jit(solution)/shard_map/psum | solution.py:64
  189.8 5.9 %all-reduce.4 = (f32[]{:T(128)}, f32[]{:T(128)}) all-reduce(f32[]{:T(128)} %get-tuple-element.12, f32[]{:T(128)} %get-tuple-element.13), channel_id=1, replica_groups=mesh['feat_0'=8,'feat_1'=4,'feat_2'=2,'row'=2,'col'=2] {'feat_2'}, use_global_device_ids=true, to_apply=%region_26.27 | all-reduce | flops 2 | bytes 16 | tf_op jit(solution)/shard_map/psum | solution.py:64
  195.7 4.5 %all-reduce.3 = (f32[]{:T(128)}, f32[]{:T(128)}) all-reduce(f32[]{:T(128)} %get-tuple-element.18, f32[]{:T(128)} %get-tuple-element.19), channel_id=1, replica_groups=mesh['feat_0'=8,'feat_1'=4,'feat_2'=2,'row'=2,'col'=2] {'row'}, use_global_device_ids=true, to_apply=%region_27.28 | all-reduce | flops 2 | bytes 16 | tf_op jit(solution)/shard_map/psum | solution.py:64
  200.1 11.6 %all-reduce.2 = (f32[]{:T(128)}, f32[]{:T(128)}) all-reduce(f32[]{:T(128)} %get-tuple-element.16, f32[]{:T(128)} %get-tuple-element.17), channel_id=1, replica_groups=mesh['feat_0'=8,'feat_1'=4,'feat_2'=2,'row'=2,'col'=2] {'col'}, use_global_device_ids=true, to_apply=%region_28.29 | all-reduce | flops 2 | bytes 16 | tf_op jit(solution)/shard_map/psum | solution.py:64
  213.0 0.6 pad_maximum_fusion
  (58 shorter events, 0.9 us)
Async XLA Ops:
  0.6 2.4 %copy-start.5 = (s32[1,4,512]{2,1,0:T(4,128)S(1)}, s32[1,4,512]{2,1,0:T(4,128)}, u32[]{:S(2)}) copy-start(s32[1,4,512]{2,1,0:T(4,128)} %param.10) | copy-start | bytes 24580
  0.6 45.8 %copy-start.1 = (s32[1,16384]{1,0:T(1,128)S(1)}, s32[1,16384]{1,0:T(1,128)}, u32[]{:S(2)}) copy-start(s32[1,16384]{1,0:T(1,128)} %param.11) | copy-start | bytes 196612
  14.8 26.2 %all-to-all-start = ((f32[64,1,256]{2,1,0:T(1,128)}), f32[64,1,256]{2,1,0:T(1,128)S(1)}, u32[]{:S(2)}, u32[]{:S(2)}) async-start(f32[64,1,256]{2,1,0:T(1,128)} %bitcast.4), calls=%async_computation | async-start | bytes 131072 | tf_op jit(solution)/shard_map/all_to_all | solution.py:46
  41.8 15.6 %all-to-all-start.1 = ((f32[64,1,256]{2,1,0:T(1,128)}), f32[64,1,256]{2,1,0:T(1,128)S(1)}, u32[]{:S(2)}, u32[]{:S(2)}) async-start(f32[64,1,256]{2,1,0:T(1,128)} %broadcast_in_dim.10), calls=%async_computation.1 | async-start | bytes 131072 | tf_op jit(solution)/shard_map/all_to_all | solution.py:25
  69.3 13.1 %copy-start = (bf16[1,4,512,256]{3,2,1,0:T(8,128)(2,1)S(1)}, bf16[1,4,512,256]{3,2,1,0:T(8,128)(2,1)}, u32[]{:S(2)}) copy-start(bf16[1,4,512,256]{3,2,1,0:T(8,128)(2,1)} %param.9) | copy-start | bytes 3145732
  82.7 0.9 copy-start.2
  82.7 1.0 copy-start.3
  82.7 1.0 copy-start.4
  157.3 56.2 %copy-start.7 = (f32[4,256]{1,0:T(4,128)}, f32[4,256]{1,0:T(4,128)S(1)}, u32[]{:S(2)}) copy-start(f32[4,256]{1,0:T(4,128)S(1)} %get-tuple-element.22) | copy-start | bytes 12292
  169.2 44.4 %copy-start.6 = (f32[4,256]{1,0:T(4,128)}, f32[4,256]{1,0:T(4,128)S(1)}, u32[]{:S(2)}) copy-start(f32[4,256]{1,0:T(4,128)S(1)} %get-tuple-element.20) | copy-start | bytes 12292
where the time goes:
time: 214 us
  blocking collectives  81.9 us (38%)
  local copies, waits for them, and re-layouts  50.6 us (24%)
  other arithmetic  28.1 us (13%)
  waiting for transfers between devices  21.9 us (10%)
  starting transfers between devices  19.7 us (9%)
  matrix products  8.28 us (4%)
  between operations  3 us (1%)
    psum x5, blocking collectives, by_axis(): x = lax.psum(x, axis)  41.2 us
    gather x2, local copies, waits for them, and re-layouts, local(): misfit_rows = misfit[index_rows].astype(jnp.bfloat16)  26.2 us
    all_to_all x2, blocking collectives, copy_for_each(): return lax.all_to_all(copies, axis, split_axis=0, concat_axis=0, tiled=True)  25.9 us
    gather x4, local copies, waits for them, and re-layouts, local(): weights[index_rows][:, :, None]  23.6 us
    scatter-add x2, other arithmetic, local(): jax.ops.segment_sum(partial_value.reshape(-1), flat_index, num_segments=s...  23.1 us
    all_to_all x1, starting transfers between devices, summed_on_arrival(): parts = lax.all_to_all(cut_along(x, dim, size), axis, 0, 0, tiled=True)  15.1 us
    all_to_all x1, blocking collectives, summed_on_arrival(): parts = lax.all_to_all(cut_along(x, dim, size), axis, 0, 0, tiled=True)  14.8 us
    all_to_all x1, waiting for transfers between devices, summed_on_arrival(): parts = lax.all_to_all(cut_along(x, dim, size), axis, 0, 0, tiled=True)  11 us
  transfers between devices with their start and end apart: 2, of which 2 were waited for; matrix products, arithmetic and copies ran while one was open for 0% of the time, Pallas kernels for 0%

commit v1 on v0

v1 whole, which is shorter than its diff:
```python
import jax
import jax.numpy as jnp
from jax import lax
from jax.experimental import pallas as pl
from jax.experimental.pallas import tpu as pltpu
from jax.sharding import Mesh
from jax.sharding import PartitionSpec as P

CG_STEPS = 3
FEAT = ("feat_0", "feat_1", "feat_2")
SHARD = ("row", "col")
LANES = 128
HIGH = 64
LOW = 256
INTERPRET = False

penalty = 1.0
damping = 0.5
threshold = 0.05


def call(kernel, *outs):
    return pl.pallas_call(
        kernel,
        out_shape=tuple(jax.ShapeDtypeStruct(shape, jnp.float32) for shape in outs),
        interpret=INTERPRET,
    )


def dot(a, b, dims):
    return lax.dot_general(a, b, (dims, ((), ())), preferred_element_type=jnp.float32)


NN = ((1,), (0,))
NT = ((1,), (1,))


def three_parts(x):
    first = x.astype(jnp.bfloat16).astype(jnp.float32)
    rest = x - first
    second = rest.astype(jnp.bfloat16).astype(jnp.float32)
    return first, second, rest - second


def low_hot(index):
    low = (index & 127) | ((index >> 13) << 7)
    places = lax.broadcasted_iota(jnp.int32, (LOW, index.shape[1]), 0)
    return jnp.where(places == low, 1.0, 0.0).astype(jnp.bfloat16)


def high_mask(index):
    high = (index >> 7) & (HIGH - 1)
    places = lax.broadcasted_iota(jnp.int32, (HIGH, index.shape[1]), 0)
    return places == high


def as_table(lines):
    return jnp.concatenate([lines[:HIGH], lines[HIGH:]], axis=1)


def scattered(x, blk_ref, hots, masks, out_ref):
    rounded = x.astype(jnp.bfloat16)
    table = None
    for b, (hot, mask) in enumerate(zip(hots, masks)):
        partial = dot(rounded, blk_ref[b], NT)[b : b + 1]
        parts = [jnp.where(mask, part, 0.0) for part in three_parts(partial)]
        spread = jnp.concatenate(parts, axis=0).astype(jnp.bfloat16)
        added = dot(spread, hot, NT)
        table = added if table is None else table + added
    table = table[:HIGH] + table[HIGH : 2 * HIGH] + table[2 * HIGH :]
    out_ref[:HIGH, :] = table[:, :LANES]
    out_ref[HIGH:, :] = table[:, LANES:]


def newton_step(x, target, margins, labels, blk_ref, hots, masks):
    blocks, size = x.shape
    parts = three_parts(as_table(margins)) + (as_table(labels.astype(jnp.float32)),)
    tables = jnp.concatenate(parts, axis=0).astype(jnp.bfloat16)
    rows = lax.broadcasted_iota(jnp.int32, (size, size), 0)
    cols = lax.broadcasted_iota(jnp.int32, (size, size), 1)
    identity = jnp.where(rows == cols, 1.0, 0.0)
    gradients = []
    hessians = []
    for b, (hot, mask) in enumerate(zip(hots, masks)):
        block = blk_ref[b]
        found = dot(tables, hot, NN)
        margin = found[:HIGH] + found[HIGH : 2 * HIGH] + found[2 * HIGH : 3 * HIGH]
        margin = jnp.sum(jnp.where(mask, margin, 0.0), axis=0, keepdims=True)
        label = jnp.sum(jnp.where(mask, found[3 * HIGH :], 0.0), axis=0, keepdims=True)
        prob = 1.0 / (1.0 + jnp.exp(-margin))
        misfit = (prob - label).astype(jnp.bfloat16)
        weight = prob * (1.0 - prob)
        gradients.append(dot(misfit, block, NN))
        turned = dot(identity.astype(jnp.bfloat16), block, NT)
        weighted = (turned * weight).astype(jnp.bfloat16)
        hessians.append(dot(weighted, block, NN) + penalty * identity)
    gradient = jnp.concatenate(gradients, axis=0) + penalty * (x - target)
    delta = jnp.zeros_like(gradient)
    residual = gradient
    direction = gradient
    power = jnp.sum(residual * residual, axis=1, keepdims=True)
    for cg_step in range(CG_STEPS):
        column = jnp.transpose(jnp.concatenate([direction, direction], axis=0))
        image = jnp.concatenate(
            [
                jnp.sum(hessians[b] * column[:, b : b + 1], axis=0, keepdims=True)
                for b in range(blocks)
            ],
            axis=0,
        )
        alpha = power / jnp.sum(direction * image, axis=1, keepdims=True)
        delta = delta + alpha * direction
        residual = residual - alpha * image
        power_next = jnp.sum(residual * residual, axis=1, keepdims=True)
        direction = residual + (power_next / power) * direction
        power = power_next
    return x - damping * delta


def hot_rows(idx_ref):
    rows = [idx_ref[b : b + 1, :] for b in range(idx_ref.shape[0])]
    return [low_hot(row) for row in rows], [high_mask(row) for row in rows]


def first_kernel(x_ref, blk_ref, idx_ref, out_ref):
    hots, masks = hot_rows(idx_ref)
    scattered(x_ref[...], blk_ref, hots, masks, out_ref)


def middle_kernel(x_ref, dual_ref, old_ref, margin_ref, label_ref, blk_ref, idx_ref, x_out, out_ref):
    hots, masks = hot_rows(idx_ref)
    target = old_ref[...] - dual_ref[...]
    x = newton_step(x_ref[...], target, margin_ref[...], label_ref[...], blk_ref, hots, masks)
    x_out[...] = x
    scattered(x, blk_ref, hots, masks, out_ref)


def last_kernel(x_ref, dual_ref, old_ref, margin_ref, label_ref, blk_ref, idx_ref, x_out, both_ref):
    hots, masks = hot_rows(idx_ref)
    dual = dual_ref[...]
    target = old_ref[...] - dual
    x = newton_step(x_ref[...], target, margin_ref[...], label_ref[...], blk_ref, hots, masks)
    x_out[...] = x
    both = jnp.concatenate([x, dual], axis=0)
    for shard in range(both_ref.shape[0]):
        both_ref[shard] = both


def consensus_kernel(both_ref, x_ref, dual_ref, old_ref, cons_ref, dual_out, sums_ref):
    shards, lines, size = both_ref.shape
    blocks = lines // 2
    solved = [both_ref[i][:blocks] for i in range(shards)]
    total = solved[0] + both_ref[0][blocks:]
    for i in range(1, shards):
        total = total + (solved[i] + both_ref[i][blocks:])
    averaged = total / float(shards)
    cut = jnp.maximum(jnp.abs(averaged) - threshold, 0.0)
    consensus = jnp.where(averaged < 0.0, -cut, cut)
    cons_ref[...] = consensus
    dual_out[...] = dual_ref[...] + x_ref[...] - consensus
    primal = jnp.zeros_like(consensus)
    for i in range(shards):
        primal = primal + (solved[i] - consensus) ** 2
    change = (consensus - old_ref[...]) ** 2
    primal = jnp.sum(jnp.sum(primal, axis=1, keepdims=True), axis=0, keepdims=True)
    change = jnp.sum(jnp.sum(change, axis=1, keepdims=True), axis=0, keepdims=True)
    lane = lax.broadcasted_iota(jnp.int32, (1, LANES), 1)
    sums = jnp.where(lane == 0, primal, jnp.where(lane == 1, float(shards) * change, 0.0))
    sums_ref[...] = jnp.broadcast_to(sums, sums_ref.shape)


def exchanged(x, axis):
    return lax.all_to_all(x, axis, 0, 0, tiled=True)


def total_of(lines):
    size = lax.axis_size(FEAT)
    parts = exchanged(lines.reshape(size, -1, LANES), FEAT)
    own = jnp.sum(parts, axis=0)
    whole = exchanged(jnp.broadcast_to(own[None], parts.shape), FEAT)
    return whole.reshape(lines.shape)


def local(local_x, dual_var, consensus_old, blocks_data, row_index, labels):
    x = local_x[0]
    dual = dual_var[0]
    blocks = blocks_data[0]
    index = row_index[0]
    marks = labels.reshape(-1, LANES)
    lines = marks.shape
    feats = lax.axis_size(FEAT)
    shards = lax.axis_size(SHARD)
    (terms,) = call(first_kernel, lines)(x, blocks, index)
    margins = total_of(terms)
    x, terms = call(middle_kernel, x.shape, lines)(
        x, dual, consensus_old, margins, marks, blocks, index
    )
    margins = total_of(terms)
    x, both = call(last_kernel, x.shape, (shards, 2 * x.shape[0], x.shape[1]))(
        x, dual, consensus_old, margins, marks, blocks, index
    )
    both = exchanged(both, SHARD)
    consensus, dual_next, sums = call(consensus_kernel, x.shape, x.shape, (feats, LANES))(
        both, x, dual, consensus_old
    )
    sums = jnp.sum(exchanged(sums.reshape(feats, 1, LANES), FEAT), axis=(0, 1))
    norms = jnp.sqrt(sums[:2]) * jnp.array([1.0, penalty], jnp.float32)
    return (x[None], dual_next[None], consensus, norms)


def solution(mesh):
    if mesh.shape["feat"] == 64:
        feat = (8, 4, 2)
    else:
        feat = (mesh.shape["feat"], 1, 1)
    torus = Mesh(
        mesh.devices.reshape(*feat, mesh.shape["row"], mesh.shape["col"]), FEAT + SHARD
    )
    placed = (
        P(SHARD, FEAT, None),
        P(SHARD, FEAT, None),
        P(FEAT, None),
        P(SHARD, FEAT, None, None),
        P(SHARD, FEAT, None),
        P(SHARD, None),
    )
    return jax.shard_map(
        local,
        mesh=torus,
        in_specs=placed,
        out_specs=(P(SHARD, FEAT, None), P(SHARD, FEAT, None), P(FEAT, None), P()),
        check_vma=False,
    )
```

time: 214 us -> 118 us (0.55)
  local copies, waits for them, and re-layouts: 50.6 us -> 0.57 us
  other arithmetic: 28.1 us -> 0.24 us
  waiting for transfers between devices: 21.9 us -> 0 us
  starting transfers between devices: 19.7 us -> 0 us
  blocking collectives: 81.9 us -> 101 us
  Pallas kernels: 0 us -> 15.3 us
  matrix products: 8.28 us -> 0 us
  between operations: 3 us -> 0.64 us
    all_to_all x3 -> x6, blocking collectives: 40.7 us -> 101 us  [exchanged(): return lax.all_to_all(x, axis, 0, 0, tiled=True)]
    gather x6 -> x0, local copies, waits for them, and re-layouts: 49.7 us -> none  [the longest x2 26.2 us: local(): misfit_rows = misfit[index_rows].astype(jnp.bfloat16)]
    psum x5 -> x0, blocking collectives: 41.2 us -> none  [by_axis(): x = lax.psum(x, axis)]
    scatter-add x2 -> x0, other arithmetic: 23.1 us -> none  [local(): jax.ops.segment_sum(partial_value.reshape(-1), flat_index, num_segments=s...]
    all_to_all x2 -> x0, waiting for transfers between devices: 21.9 us -> none  [the longest x1 11 us: summed_on_arrival(): parts = lax.all_to_all(cut_along(x, dim, size), axis, 0, 0, tiled=True)]
    all_to_all x2 -> x0, starting transfers between devices: 19.7 us -> none  [the longest x1 15.1 us: summed_on_arrival(): parts = lax.all_to_all(cut_along(x, dim, size), axis, 0, 0, tiled=True)]
    pallas_call x0 -> x4, Pallas kernels: none -> 15.3 us  [the longest x1 6 us: local(): call(middle_kernel, x.shape, lines)]
    dot_general x12 -> x0, matrix products: 8.28 us -> none  [the longest x6 3.96 us: conjugate_solve(): jnp.einsum('bkl,bl->bk', hessian, direction, precision=lax.Precision.HIGH...]
  transfers between devices with their start and end apart: 2 -> 0, of which waited for: 2 -> 0; matrix products, arithmetic and copies ran while one was open for 0% -> 0% of each run, Pallas kernels for 0% -> 0%
where the time goes in v1:
time: 118 us
  blocking collectives  101 us (86%)
  Pallas kernels  15.3 us (13%)
    all_to_all x6, blocking collectives, exchanged(): return lax.all_to_all(x, axis, 0, 0, tiled=True)  101 us
    pallas_call x1, Pallas kernels, local(): call(middle_kernel, x.shape, lines)  6 us
    pallas_call x1, Pallas kernels, local(): call(last_kernel, x.shape, (shards, 2 * x.shape[0], x.shape[1]))  5 us
    pallas_call x1, Pallas kernels, local(): terms, = call(first_kernel, lines)(x, blocks, index)  2.84 us

profile of v1, /device:TPU:1, one launch (start us, length us, event | category | flops | bytes accessed | tf_op | source)
XLA Modules:
  0.0 117.7 jit_solution(9029578516495745243)
XLA Ops:
  0.6 2.8 %shard_map.102 = f32[128,128]{1,0:T(8,128)} custom-call(f32[4,256]{1,0:T(4,128)} %bitcast.30, bf16[4,512,256]{2,1,0:T(8,128)(2,1)} %bitcast.14, s32[4,512]{1,0:T(4,128)} %bitcast.22), custom_call_target="tpu_custom_call" | custom-call | tf_op jit(solution)/shard_map/pallas_call | solution.py:193
  3.5 26.2 %all_to_all.30 = f32[64,2,128]{2,1,0:T(2,128)S(1)} all-to-all(f32[64,2,128]{2,1,0:T(2,128)} %bitcast.21), channel_id=1, replica_groups=mesh['feat_0'=8,'feat_1'=4,'feat_2'=2,'row'=2,'col'=2] {'feat_0','feat_1..., dimensions={0} | all-to-all | bytes 131072 | tf_op jit(solution)/shard_map/all_to_all | solution.py:173
  29.6 0.1 reduce_sum.27
  29.7 15.5 %all_to_all.31 = f32[64,2,128]{2,1,0:T(2,128)} all-to-all(f32[64,2,128]{2,1,0:T(2,128)S(1)} %broadcast_in_dim.8), channel_id=1, replica_groups=mesh['feat_0'=8,'feat_1'=4,'feat_2'=2,'row'=2,'col'=2] {'feat_0','feat_1..., dimensions={0} | all-to-all | bytes 131072 | tf_op jit(solution)/shard_map/all_to_all | solution.py:173
  45.2 6.0 %shard_map.103 = (f32[4,256]{1,0:T(4,128)}, f32[128,128]{1,0:T(8,128)}) custom-call(f32[4,256]{1,0:T(4,128)} %bitcast.31, f32[4,256]{1,0:T(4,128)} %bitcast.26, f32[4,256]{1,0:T(4,128)} %old_ref.5, f32[128,128]{1,0:T(8,128)} %bitcast.20, s32[128,128]{1,0:T(8,128)} %bitcast.17, bf16[4,512,256]{2,1,0:T(8,128)(2,1)} %bitcast.15, s32[4,512]{1,0:T(4,128)} %bitcast.23), custom_call_target="tpu_custom_call" | custom-call | tf_op jit(solution)/shard_map/pallas_call | solution.py:195
  51.2 15.6 %all_to_all.32 = f32[64,2,128]{2,1,0:T(2,128)S(1)} all-to-all(f32[64,2,128]{2,1,0:T(2,128)} %bitcast.25), channel_id=1, replica_groups=mesh['feat_0'=8,'feat_1'=4,'feat_2'=2,'row'=2,'col'=2] {'feat_0','feat_1..., dimensions={0} | all-to-all | bytes 131072 | tf_op jit(solution)/shard_map/all_to_all | solution.py:173
  66.8 0.1 reduce_sum.28
  66.9 15.5 %all_to_all.33 = f32[64,2,128]{2,1,0:T(2,128)} all-to-all(f32[64,2,128]{2,1,0:T(2,128)S(1)} %broadcast_in_dim.9), channel_id=1, replica_groups=mesh['feat_0'=8,'feat_1'=4,'feat_2'=2,'row'=2,'col'=2] {'feat_0','feat_1..., dimensions={0} | all-to-all | bytes 131072 | tf_op jit(solution)/shard_map/all_to_all | solution.py:173
  82.4 5.0 %shard_map.104 = (f32[4,256]{1,0:T(4,128)}, f32[4,8,256]{2,1,0:T(8,128)}) custom-call(f32[4,256]{1,0:T(4,128)} %get-tuple-element.11.x_ref, f32[4,256]{1,0:T(4,128)} %bitcast.27, f32[4,256]{1,0:T(4,128)} %old_ref.5, f32[128,128]{1,0:T(8,128)} %bitcast.19, s32[128,128]{1,0:T(8,128)} %bitcast.18, bf16[4,512,256]{2,1,0:T(8,128)(2,1)} %bitcast.16, s32[4,512]{1,0:T(4,128)} %bitcast.24), custom_call_target="tpu_custom_call" | custom-call | tf_op jit(solution)/shard_map/pallas_call | solution.py:199
  87.4 12.7 %all_to_all.34.both_ref = f32[4,8,256]{2,1,0:T(8,128)} all-to-all(f32[4,8,256]{2,1,0:T(8,128)} %get-tuple-element.14), channel_id=1, replica_groups=mesh['feat_0'=8,'feat_1'=4,'feat_2'=2,'row'=2,'col'=2] {'row','col'}, dimensions={0} | all-to-all | bytes 65536 | tf_op jit(solution)/shard_map/all_to_all | solution.py:173
  100.1 1.5 %shard_map.105 = (f32[4,256]{1,0:T(4,128)}, f32[4,256]{1,0:T(4,128)}, f32[64,128]{1,0:T(8,128)}) custom-call(f32[4,8,256]{2,1,0:T(8,128)} %all_to_all.34.both_ref, f32[4,256]{1,0:T(4,128)} %get-tuple-element.13.x_ref, f32[4,256]{1,0:T(4,128)} %bitcast.28, f32[4,256]{1,0:T(4,128)} %old_ref.5), custom_call_target="tpu_custom_call" | custom-call | tf_op jit(solution)/shard_map/pallas_call | solution.py:203
  101.6 15.5 %all_to_all.35 = f32[64,1,128]{2,1,0:T(1,128)S(1)} all-to-all(f32[64,1,128]{2,1,0:T(1,128)} %bitcast.29), channel_id=1, replica_groups=mesh['feat_0'=8,'feat_1'=4,'feat_2'=2,'row'=2,'col'=2] {'feat_0','feat_1..., dimensions={0} | all-to-all | bytes 65536 | tf_op jit(solution)/shard_map/all_to_all | solution.py:173
  117.1 0.1 reduce_sum.29
  117.2 0.5 slice_sqrt_fusion
  (2 shorter events, 0.0 us)

commit v2 on v1

--- a/solution.py
+++ b/solution.py
@@ -9,9 +9,12 @@
 CG_STEPS = 3
 FEAT = ("feat_0", "feat_1", "feat_2")
 SHARD = ("row", "col")
+NEAR = ("feat_2", "row", "col")
+FAR = ("feat_0", "feat_1")
 LANES = 128
 HIGH = 64
 LOW = 256
+SHARDS = 4
 INTERPRET = False
 
 penalty = 1.0
@@ -19,12 +22,18 @@
 threshold = 0.05
 
 
+def in_vmem(*args):
+    if INTERPRET:
+        return args
+    return [pltpu.with_memory_space_constraint(arg, pltpu.VMEM) for arg in args]
+
+
 def call(kernel, *outs):
-    return pl.pallas_call(
-        kernel,
-        out_shape=tuple(jax.ShapeDtypeStruct(shape, jnp.float32) for shape in outs),
-        interpret=INTERPRET,
-    )
+    if INTERPRET:
+        shapes = tuple(jax.ShapeDtypeStruct(shape, jnp.float32) for shape in outs)
+    else:
+        shapes = tuple(pltpu.VMEM(shape, jnp.float32) for shape in outs)
+    return pl.pallas_call(kernel, out_shape=shapes, interpret=INTERPRET)
 
 
 def dot(a, b, dims):
@@ -135,37 +144,54 @@
     scattered(x, blk_ref, hots, masks, out_ref)
 
 
-def last_kernel(x_ref, dual_ref, old_ref, margin_ref, label_ref, blk_ref, idx_ref, x_out, both_ref):
+def last_kernel(x_ref, dual_ref, old_ref, margin_ref, label_ref, blk_ref, idx_ref, x_out, sent_ref):
     hots, masks = hot_rows(idx_ref)
     dual = dual_ref[...]
-    target = old_ref[...] - dual
-    x = newton_step(x_ref[...], target, margin_ref[...], label_ref[...], blk_ref, hots, masks)
+    old = old_ref[...]
+    x = newton_step(x_ref[...], old - dual, margin_ref[...], label_ref[...], blk_ref, hots, masks)
     x_out[...] = x
-    both = jnp.concatenate([x, dual], axis=0)
-    for shard in range(both_ref.shape[0]):
-        both_ref[shard] = both
-
-
-def consensus_kernel(both_ref, x_ref, dual_ref, old_ref, cons_ref, dual_out, sums_ref):
-    shards, lines, size = both_ref.shape
-    blocks = lines // 2
-    solved = [both_ref[i][:blocks] for i in range(shards)]
-    total = solved[0] + both_ref[0][blocks:]
-    for i in range(1, shards):
-        total = total + (solved[i] + both_ref[i][blocks:])
-    averaged = total / float(shards)
-    cut = jnp.maximum(jnp.abs(averaged) - threshold, 0.0)
-    consensus = jnp.where(averaged < 0.0, -cut, cut)
+    sent = jnp.concatenate([x, dual, old, jnp.zeros_like(old)], axis=0)
+    for peer in range(sent_ref.shape[0]):
+        sent_ref[peer] = sent
+
+
+def full_sum(values):
+    return jnp.sum(jnp.sum(values, axis=1, keepdims=True), axis=0, keepdims=True)
+
+
+def consensus_kernel(came_ref, place_ref, x_ref, dual_ref, cons_ref, dual_out, sums_ref):
+    blocks = x_ref.shape[0]
+    groups = came_ref.shape[0] // SHARDS
+    primal = change = None
+    found = []
+    for group in range(groups):
+        came = [came_ref[group * SHARDS + i] for i in range(SHARDS)]
+        solved = [each[:blocks] for each in came]
+        old = came[0][2 * blocks : 3 * blocks]
+        total = solved[0] + came[0][blocks : 2 * blocks]
+        for i in range(1, SHARDS):
+            total = total + (solved[i] + came[i][blocks : 2 * blocks])
+        averaged = total / float(SHARDS)
+        cut = jnp.maximum(jnp.abs(averaged) - threshold, 0.0)
+        consensus = jnp.where(averaged < 0.0, -cut, cut)
+        found.append(consensus)
+        squares = [(each - consensus) ** 2 for each in solved]
+        for square in squares:
+            primal = square if primal is None else primal + square
+        moved = (consensus - old) ** 2
+        change = moved if change is None else change + moved
+    consensus = found[0]
+    for group in range(1, groups):
+        own = jnp.broadcast_to(place_ref[:1, :1], consensus.shape) == float(group)
+        consensus = jnp.where(own, found[group], consensus)
     cons_ref[...] = consensus
     dual_out[...] = dual_ref[...] + x_ref[...] - consensus
-    primal = jnp.zeros_like(consensus)
-    for i in range(shards):
-        primal = primal + (solved[i] - consensus) ** 2
-    change = (consensus - old_ref[...]) ** 2
-    primal = jnp.sum(jnp.sum(primal, axis=1, keepdims=True), axis=0, keepdims=True)
-    change = jnp.sum(jnp.sum(change, axis=1, keepdims=True), axis=0, keepdims=True)
     lane = lax.broadcasted_iota(jnp.int32, (1, LANES), 1)
-    sums = jnp.where(lane == 0, primal, jnp.where(lane == 1, float(shards) * change, 0.0))
+    sums = jnp.where(
+        lane == 0,
+        full_sum(primal),
+        jnp.where(lane == 1, float(SHARDS) * full_sum(change), 0.0),
+    )
     sums_ref[...] = jnp.broadcast_to(sums, sums_ref.shape)
 
 
@@ -188,22 +214,24 @@
     index = row_index[0]
     marks = labels.reshape(-1, LANES)
     lines = marks.shape
-    feats = lax.axis_size(FEAT)
-    shards = lax.axis_size(SHARD)
+    lanes, size = x.shape
+    near = lax.axis_size(NEAR)
+    far = lax.axis_size(FAR)
+    place = jnp.full((8, LANES), lax.axis_index("feat_2"), jnp.float32)
     (terms,) = call(first_kernel, lines)(x, blocks, index)
     margins = total_of(terms)
     x, terms = call(middle_kernel, x.shape, lines)(
-        x, dual, consensus_old, margins, marks, blocks, index
+        *in_vmem(x, dual, consensus_old, margins, marks, blocks, index)
     )
     margins = total_of(terms)
-    x, both = call(last_kernel, x.shape, (shards, 2 * x.shape[0], x.shape[1]))(
-        x, dual, consensus_old, margins, marks, blocks, index
-    )
-    both = exchanged(both, SHARD)
-    consensus, dual_next, sums = call(consensus_kernel, x.shape, x.shape, (feats, LANES))(
-        both, x, dual, consensus_old
-    )
-    sums = jnp.sum(exchanged(sums.reshape(feats, 1, LANES), FEAT), axis=(0, 1))
+    x, sent = call(last_kernel, x.shape, (near, 4 * lanes, size))(
+        *in_vmem(x, dual, consensus_old, margins, marks, blocks, index)
+    )
+    came = exchanged(sent, NEAR)
+    consensus, dual_next, sums = call(consensus_kernel, x.shape, x.shape, (far, LANES))(
+        *in_vmem(came, place, x, dual)
+    )
+    sums = jnp.sum(exchanged(sums.reshape(far, 1, LANES), FAR), axis=(0, 1))
     norms = jnp.sqrt(sums[:2]) * jnp.array([1.0, penalty], jnp.float32)
     return (x[None], dual_next[None], consensus, norms)
 
@@ -212,7 +240,7 @@
     if mesh.shape["feat"] == 64:
         feat = (8, 4, 2)
     else:
-        feat = (mesh.shape["feat"], 1, 1)
+        feat = (mesh.shape["feat"] // 2, 1, 2)
     torus = Mesh(
         mesh.devices.reshape(*feat, mesh.shape["row"], mesh.shape["col"]), FEAT + SHARD
     )

time: 118 us -> 110 us (0.932)
  blocking collectives: 101 us -> 70.4 us
  starting transfers between devices: 0 us -> 12.7 us
  waiting for transfers between devices: 0 us -> 11.9 us
  Pallas kernels: 15.3 us -> 10.9 us
  local copies, waits for them, and re-layouts: 0.57 us -> 3.03 us
    all_to_all x6 -> x4, blocking collectives: 101 us -> 70.4 us  [exchanged(): return lax.all_to_all(x, axis, 0, 0, tiled=True)]
    all_to_all x0 -> x2, starting transfers between devices: none -> 12.7 us  [exchanged(): return lax.all_to_all(x, axis, 0, 0, tiled=True)]
    all_to_all x0 -> x2, waiting for transfers between devices: none -> 11.9 us  [exchanged(): return lax.all_to_all(x, axis, 0, 0, tiled=True)]
    unnamed x0 -> x15, local copies, waits for them, and re-layouts: none -> 2.46 us
    pallas_call x2, Pallas kernels: 6.49 us -> 4.49 us  [the longest x1 3.79 us: local(): call(last_kernel, x.shape, (near, 4 * lanes, size))]
    pallas_call x1, Pallas kernels: 6 us -> 4.12 us  [local(): call(middle_kernel, x.shape, lines)]
  transfers between devices with their start and end apart: 0 -> 2, of which waited for: 0 -> 2; matrix products, arithmetic and copies ran while one was open for 0% -> 2% of each run, Pallas kernels for 0% -> 0%
where the time goes in v2:
time: 110 us
  blocking collectives  70.4 us (64%)
  starting transfers between devices  12.7 us (12%)
  waiting for transfers between devices  11.9 us (11%)
  Pallas kernels  10.9 us (10%)
  local copies, waits for them, and re-layouts  3.03 us (3%)
    all_to_all x4, blocking collectives, exchanged(): return lax.all_to_all(x, axis, 0, 0, tiled=True)  70.4 us
    all_to_all x2, starting transfers between devices, exchanged(): return lax.all_to_all(x, axis, 0, 0, tiled=True)  12.7 us
    all_to_all x2, waiting for transfers between devices, exchanged(): return lax.all_to_all(x, axis, 0, 0, tiled=True)  11.9 us
    pallas_call x1, Pallas kernels, local(): call(middle_kernel, x.shape, lines)  4.12 us
    pallas_call x1, Pallas kernels, local(): call(last_kernel, x.shape, (near, 4 * lanes, size))  3.79 us
    unnamed x15, local copies, waits for them, and re-layouts  2.46 us
    pallas_call x1, Pallas kernels, local(): terms, = call(first_kernel, lines)(x, blocks, index)  2.3 us
  transfers between devices with their start and end apart: 2, of which 2 were waited for; matrix products, arithmetic and copies ran while one was open for 2% of the time, Pallas kernels for 0%

profile of v2, /device:TPU:1, one launch (start us, length us, event | category | flops | bytes accessed | tf_op | source)
XLA Modules:
  0.0 110.0 jit_solution(11603167454871250259)
XLA Ops:
  0.6 0.0 copy-start
  0.6 2.3 %shard_map.102 = f32[128,128]{1,0:T(8,128)S(1)} custom-call(f32[4,256]{1,0:T(4,128)} %bitcast.31, bf16[4,512,256]{2,1,0:T(8,128)(2,1)} %bitcast.16, s32[4,512]{1,0:T(4,128)} %bitcast.24), custom_call_target="tpu_custom_call" | custom-call | tf_op jit(solution)/shard_map/pallas_call | solution.py:221
  2.9 26.0 %all_to_all.30 = f32[64,2,128]{2,1,0:T(2,128)S(1)} all-to-all(f32[64,2,128]{2,1,0:T(2,128)S(1)} %bitcast.23), channel_id=1, replica_groups=mesh['feat_0'=8,'feat_1'=4,'feat_2'=2,'row'=2,'col'=2] {'feat_0','feat_1..., dimensions={0} | all-to-all | bytes 131072 | tf_op jit(solution)/shard_map/all_to_all | solution.py:199
  28.9 0.1 reduce_sum.27
  29.0 0.0 copy-start.1
  29.0 0.0 copy-start.2
  29.0 0.0 copy-start.4
  29.1 0.0 copy-start.5
  29.1 14.9 %all_to_all.31 = f32[64,2,128]{2,1,0:T(2,128)S(1)} all-to-all(f32[64,2,128]{2,1,0:T(2,128)S(1)} %broadcast_in_dim.10), channel_id=1, replica_groups=mesh['feat_0'=8,'feat_1'=4,'feat_2'=2,'row'=2,'col'=2] {'feat_0','feat_1..., dimensions={0} | all-to-all | bytes 131072 | tf_op jit(solution)/shard_map/all_to_all | solution.py:199
  44.0 0.0 copy-start.3
  44.0 0.0 copy-done
  44.0 0.0 copy-done.1
  44.0 0.0 copy-done.2
  44.0 0.0 copy-done.4
  44.0 0.0 copy-done.5
  44.0 0.7 copy-done.3
  44.7 4.1 %shard_map.103 = (f32[4,256]{1,0:T(4,128)S(1)}, f32[128,128]{1,0:T(8,128)S(1)}) custom-call(f32[4,256]{1,0:T(4,128)S(1)} %bitcast.32, f32[4,256]{1,0:T(4,128)S(1)} %bitcast.28, f32[4,256]{1,0:T(4,128)S(1)} %copy-done.5, f32[128,128]{1,0:T(8,128)S(1)} %bitcast.22, s32[128,128]{1,0:T(8,128)S(1)} %bitcast.19, bf16[4,512,256]{2,1,0:T(8,128)(2,1)S(1)} %bitcast.17, ...), custom_call_target="tpu_custom_call" | custom-call | tf_op jit(solution)/shard_map/pallas_call | solution.py:223
  48.8 14.8 %all_to_all.32 = f32[64,2,128]{2,1,0:T(2,128)S(1)} all-to-all(f32[64,2,128]{2,1,0:T(2,128)S(1)} %bitcast.27), channel_id=1, replica_groups=mesh['feat_0'=8,'feat_1'=4,'feat_2'=2,'row'=2,'col'=2] {'feat_0','feat_1..., dimensions={0} | all-to-all | bytes 131072 | tf_op jit(solution)/shard_map/all_to_all | solution.py:199
  63.6 0.1 reduce_sum.28
  63.7 14.8 %all_to_all.33 = f32[64,2,128]{2,1,0:T(2,128)S(1)} all-to-all(f32[64,2,128]{2,1,0:T(2,128)S(1)} %broadcast_in_dim.22), channel_id=1, replica_groups=mesh['feat_0'=8,'feat_1'=4,'feat_2'=2,'row'=2,'col'=2] {'feat_0','feat_1..., dimensions={0} | all-to-all | bytes 131072 | tf_op jit(solution)/shard_map/all_to_all | solution.py:199
  78.5 3.8 %shard_map.104 = (f32[4,256]{1,0:T(4,128)S(1)}, f32[8,16,256]{2,1,0:T(8,128)}) custom-call(f32[4,256]{1,0:T(4,128)S(1)} %get-tuple-element.11.x_ref, f32[4,256]{1,0:T(4,128)S(1)} %bitcast.29, f32[4,256]{1,0:T(4,128)S(1)} %copy-done.5, f32[128,128]{1,0:T(8,128)S(1)} %bitcast.21, s32[128,128]{1,0:T(8,128)S(1)} %bitcast.20, bf16[4,512,256]{2,1,0:T(8,128)(2,1)S(1)} %bitcast.18, ...), custom_call_target="tpu_custom_call" | custom-call | tf_op jit(solution)/shard_map/pallas_call | solution.py:227
  82.3 8.9 %all-to-all-start.4 = ((f32[8,16,256]{2,1,0:T(8,128)}), f32[8,16,256]{2,1,0:T(8,128)S(1)}, u32[]{:S(2)}, u32[]{:S(2)}) async-start(f32[8,16,256]{2,1,0:T(8,128)} %get-tuple-element.14), calls=%async_computation.4 | async-start | bytes 262144 | tf_op jit(solution)/shard_map/all_to_all | solution.py:199
  91.2 5.3 %all-to-all-done.4.came_ref = f32[8,16,256]{2,1,0:T(8,128)S(1)} async-done(((f32[8,16,256]{2,1,0:T(8,128)}), f32[8,16,256]{2,1,0:T(8,128)S(1)}, u32[]{:S(2)}, u32[]{:S(2)}) %all-to-all-start.4) | async-done | bytes 131104 | tf_op jit(solution)/shard_map/all_to_all | solution.py:199
  96.4 0.7 shard_map.105
  97.1 3.8 %all-to-all-start.5 = ((f32[32,1,128]{2,1,0:T(1,128)}), f32[32,1,128]{2,1,0:T(1,128)S(1)}, u32[]{:S(2)}, u32[]{:S(2)}) async-start(f32[32,1,128]{2,1,0:T(1,128)} %bitcast.12), calls=%async_computation.5 | async-start | bytes 32768 | tf_op jit(solution)/shard_map/all_to_all | solution.py:199
  100.9 0.6 copy.12
  101.5 0.6 copy.13
  102.1 0.6 copy.14
  102.7 6.7 %all-to-all-done.5 = f32[32,1,128]{2,1,0:T(1,128)S(1)} async-done(((f32[32,1,128]{2,1,0:T(1,128)}), f32[32,1,128]{2,1,0:T(1,128)S(1)}, u32[]{:S(2)}, u32[]{:S(2)}) %all-to-all-start.5) | async-done | bytes 16416 | tf_op jit(solution)/shard_map/all_to_all | solution.py:199
  109.4 0.1 reduce_sum.29
  109.4 0.5 slice_sqrt_fusion
  (3 shorter events, 0.0 us)
Async XLA Ops:
  0.6 43.4 %copy-start = (bf16[1,4,512,256]{3,2,1,0:T(8,128)(2,1)S(1)}, bf16[1,4,512,256]{3,2,1,0:T(8,128)(2,1)}, u32[]{:S(2)}) copy-start(bf16[1,4,512,256]{3,2,1,0:T(8,128)(2,1)} %param.10) | copy-start | bytes 3145732
  29.0 15.0 %copy-start.1 = (s32[1,16384]{1,0:T(1,128)S(1)}, s32[1,16384]{1,0:T(1,128)}, u32[]{:S(2)}) copy-start(s32[1,16384]{1,0:T(1,128)} %param.12) | copy-start | bytes 196612
  29.0 15.0 %copy-start.2 = (s32[1,4,512]{2,1,0:T(4,128)S(1)}, s32[1,4,512]{2,1,0:T(4,128)}, u32[]{:S(2)}) copy-start(s32[1,4,512]{2,1,0:T(4,128)} %param.11) | copy-start | bytes 24580
  29.0 15.0 %copy-start.4 = (f32[1,4,256]{2,1,0:T(4,128)S(1)}, f32[1,4,256]{2,1,0:T(4,128)}, u32[]{:S(2)}) copy-start(f32[1,4,256]{2,1,0:T(4,128)} %param.7) | copy-start | bytes 12292
  29.1 15.0 %copy-start.5 = (f32[4,256]{1,0:T(4,128)S(1)}, f32[4,256]{1,0:T(4,128)}, u32[]{:S(2)}) copy-start(f32[4,256]{1,0:T(4,128)} %old_ref.3) | copy-start | bytes 12292
  44.0 0.7 copy-start.3
  82.3 14.2 %all-to-all-start.4 = ((f32[8,16,256]{2,1,0:T(8,128)}), f32[8,16,256]{2,1,0:T(8,128)S(1)}, u32[]{:S(2)}, u32[]{:S(2)}) async-start(f32[8,16,256]{2,1,0:T(8,128)} %get-tuple-element.14), calls=%async_computation.4 | async-start | bytes 262144 | tf_op jit(solution)/shard_map/all_to_all | solution.py:199
  97.1 12.2 %all-to-all-start.5 = ((f32[32,1,128]{2,1,0:T(1,128)}), f32[32,1,128]{2,1,0:T(1,128)S(1)}, u32[]{:S(2)}, u32[]{:S(2)}) async-start(f32[32,1,128]{2,1,0:T(1,128)} %bitcast.12), calls=%async_computation.5 | async-start | bytes 32768 | tf_op jit(solution)/shard_map/all_to_all | solution.py:199

commit v3 on v2

--- a/solution.py
+++ b/solution.py
@@ -22,18 +22,37 @@
 threshold = 0.05
 
 
-def in_vmem(*args):
+HBM = pl.BlockSpec(memory_space=pltpu.HBM)
+
+
+def placed_in(space, args):
     if INTERPRET:
         return args
-    return [pltpu.with_memory_space_constraint(arg, pltpu.VMEM) for arg in args]
-
-
-def call(kernel, *outs):
+    return [pltpu.with_memory_space_constraint(arg, space) for arg in args]
+
+
+def in_vmem(*args):
+    return placed_in(pltpu.VMEM, args)
+
+
+def in_hbm(*args):
+    return placed_in(pltpu.HBM, args)
+
+
+def held(shape, kind=jnp.float32):
     if INTERPRET:
-        shapes = tuple(jax.ShapeDtypeStruct(shape, jnp.float32) for shape in outs)
-    else:
-        shapes = tuple(pltpu.VMEM(shape, jnp.float32) for shape in outs)
-    return pl.pallas_call(kernel, out_shape=shapes, interpret=INTERPRET)
+        return jax.ShapeDtypeStruct(shape, kind)
+    return pltpu.VMEM(shape, kind)
+
+
+def call(kernel, *outs, **options):
+    return pl.pallas_call(
+        kernel,
+        out_shape=outs,
+        interpret=INTERPRET,
+        compiler_params=pltpu.CompilerParams(vmem_limit_bytes=16 << 20),
+        **options,
+    )
 
 
 def dot(a, b, dims):
@@ -67,32 +86,34 @@
     return jnp.concatenate([lines[:HIGH], lines[HIGH:]], axis=1)
 
 
-def scattered(x, blk_ref, hots, masks, out_ref):
-    rounded = x.astype(jnp.bfloat16)
-    table = None
-    for b, (hot, mask) in enumerate(zip(hots, masks)):
-        partial = dot(rounded, blk_ref[b], NT)[b : b + 1]
-        parts = [jnp.where(mask, part, 0.0) for part in three_parts(partial)]
-        spread = jnp.concatenate(parts, axis=0).astype(jnp.bfloat16)
-        added = dot(spread, hot, NT)
-        table = added if table is None else table + added
+def spread(rounded, turned, hot, mask, b):
+    partial = dot(rounded, turned, NN)[b : b + 1]
+    parts = [jnp.where(mask, part, 0.0) for part in three_parts(partial)]
+    return dot(jnp.concatenate(parts, axis=0).astype(jnp.bfloat16), hot, NT)
+
+
+def put(table, out_ref):
     table = table[:HIGH] + table[HIGH : 2 * HIGH] + table[2 * HIGH :]
     out_ref[:HIGH, :] = table[:, :LANES]
     out_ref[HIGH:, :] = table[:, LANES:]
 
 
-def newton_step(x, target, margins, labels, blk_ref, hots, masks):
+def identity_of(size):
+    rows = lax.broadcasted_iota(jnp.int32, (size, size), 0)
+    cols = lax.broadcasted_iota(jnp.int32, (size, size), 1)
+    return jnp.where(rows == cols, 1.0, 0.0)
+
+
+def newton_step(x, target, margins, labels, blk_ref, turn_ref, hot_ref, masks):
     blocks, size = x.shape
     parts = three_parts(as_table(margins)) + (as_table(labels.astype(jnp.float32)),)
     tables = jnp.concatenate(parts, axis=0).astype(jnp.bfloat16)
-    rows = lax.broadcasted_iota(jnp.int32, (size, size), 0)
-    cols = lax.broadcasted_iota(jnp.int32, (size, size), 1)
-    identity = jnp.where(rows == cols, 1.0, 0.0)
+    identity = identity_of(size)
     gradients = []
     hessians = []
-    for b, (hot, mask) in enumerate(zip(hots, masks)):
+    for b, mask in enumerate(masks):
         block = blk_ref[b]
-        found = dot(tables, hot, NN)
+        found = dot(tables, hot_ref[b], NN)
         margin = found[:HIGH] + found[HIGH : 2 * HIGH] + found[2 * HIGH : 3 * HIGH]
         margin = jnp.sum(jnp.where(mask, margin, 0.0), axis=0, keepdims=True)
         label = jnp.sum(jnp.where(mask, found[3 * HIGH :], 0.0), axis=0, keepdims=True)
@@ -100,8 +121,7 @@
         misfit = (prob - label).astype(jnp.bfloat16)
         weight = prob * (1.0 - prob)
         gradients.append(dot(misfit, block, NN))
-        turned = dot(identity.astype(jnp.bfloat16), block, NT)
-        weighted = (turned * weight).astype(jnp.bfloat16)
+        weighted = (turn_ref[b].astype(jnp.float32) * weight).astype(jnp.bfloat16)
         hessians.append(dot(weighted, block, NN) + penalty * identity)
     gradient = jnp.concatenate(gradients, axis=0) + penalty * (x - target)
     delta = jnp.zeros_like(gradient)
@@ -126,29 +146,72 @@
     return x - damping * delta
 
 
-def hot_rows(idx_ref):
-    rows = [idx_ref[b : b + 1, :] for b in range(idx_ref.shape[0])]
-    return [low_hot(row) for row in rows], [high_mask(row) for row in rows]
-
-
-def first_kernel(x_ref, blk_ref, idx_ref, out_ref):
-    hots, masks = hot_rows(idx_ref)
-    scattered(x_ref[...], blk_ref, hots, masks, out_ref)
-
-
-def middle_kernel(x_ref, dual_ref, old_ref, margin_ref, label_ref, blk_ref, idx_ref, x_out, out_ref):
-    hots, masks = hot_rows(idx_ref)
+def masks_of(idx_ref):
+    return [high_mask(idx_ref[b : b + 1, :]) for b in range(idx_ref.shape[0])]
+
+
+def first_kernel(place_ref, *refs):
+    given, (table_ref, hot_ref, turn_ref, place_out, *kept), (sems, block_sems) = refs[:6], refs[6:-2], refs[-2:]
+    (idx_in, x_in, blk_in, *_), (idx_ref, x_ref, blk_ref, *_) = given, kept
+    copies = [
+        pltpu.make_async_copy(src, dst, sems.at[i])
+        for i, (src, dst) in enumerate(zip(given, kept))
+        if i != 2
+    ]
+    blocks = [
+        pltpu.make_async_copy(blk_in.at[b], blk_ref.at[b], block_sems.at[b])
+        for b in range(blk_ref.shape[0])
+    ]
+    copies[0].start()
+    copies[1].start()
+    for copy in blocks:
+        copy.start()
+    for copy in copies[2:]:
+        copy.start()
+    place_out[...] = place_ref[...]
+    copies[0].wait()
+    for b in range(blk_ref.shape[0]):
+        hot_ref[b] = low_hot(idx_ref[b : b + 1, :])
+    masks = masks_of(idx_ref)
+    identity = identity_of(x_ref.shape[1]).astype(jnp.bfloat16)
+    copies[1].wait()
+    rounded = x_ref[...].astype(jnp.bfloat16)
+    table = None
+    for b, mask in enumerate(masks):
+        blocks[b].wait()
+        turned = dot(identity, blk_ref[b], NT).astype(jnp.bfloat16)
+        turn_ref[b] = turned
+        added = spread(rounded, turned, hot_ref[b], mask, b)
+        table = added if table is None else table + added
+    put(table, table_ref)
+    for copy in copies[2:]:
+        copy.wait()
+
+
+def middle_kernel(margin_ref, hot_ref, turn_ref, idx_ref, x_ref, blk_ref, dual_ref, old_ref, label_ref, x_out, out_ref):
+    masks = masks_of(idx_ref)
     target = old_ref[...] - dual_ref[...]
-    x = newton_step(x_ref[...], target, margin_ref[...], label_ref[...], blk_ref, hots, masks)
+    x = newton_step(
+        x_ref[...], target, margin_ref[...], label_ref[...], blk_ref, turn_ref, hot_ref, masks
+    )
     x_out[...] = x
-    scattered(x, blk_ref, hots, masks, out_ref)
-
-
-def last_kernel(x_ref, dual_ref, old_ref, margin_ref, label_ref, blk_ref, idx_ref, x_out, sent_ref):
-    hots, masks = hot_rows(idx_ref)
+    rounded = x.astype(jnp.bfloat16)
+    table = None
+    for b, mask in enumerate(masks):
+        added = spread(rounded, turn_ref[b], hot_ref[b], mask, b)
+        table = added if table is None else table + added
+    put(table, out_ref)
+
+
+def last_kernel(
+    margin_ref, hot_ref, turn_ref, idx_ref, x_ref, blk_ref, dual_ref, old_ref, label_ref, x_out, sent_ref
+):
+    masks = masks_of(idx_ref)
     dual = dual_ref[...]
     old = old_ref[...]
-    x = newton_step(x_ref[...], old - dual, margin_ref[...], label_ref[...], blk_ref, hots, masks)
+    x = newton_step(
+        x_ref[...], old - dual, margin_ref[...], label_ref[...], blk_ref, turn_ref, hot_ref, masks
+    )
     x_out[...] = x
     sent = jnp.concatenate([x, dual, old, jnp.zeros_like(old)], axis=0)
     for peer in range(sent_ref.shape[0]):
@@ -195,15 +258,29 @@
     sums_ref[...] = jnp.broadcast_to(sums, sums_ref.shape)
 
 
+def finish_kernel(sums_ref, x_ref, dual_ref, cons_ref, x_out, dual_out, cons_out, norms_ref, sems):
+    pairs = ((x_ref, x_out), (dual_ref, dual_out), (cons_ref, cons_out))
+    copies = [pltpu.make_async_copy(src, dst, sems.at[i]) for i, (src, dst) in enumerate(pairs)]
+    for copy in copies:
+        copy.start()
+    sums = jnp.sqrt(jnp.sum(sums_ref[...], axis=0, keepdims=True))
+    lane = lax.broadcasted_iota(jnp.int32, sums.shape, 1)
+    norms_ref[0] = jnp.sum(jnp.where(lane == 0, sums, 0.0))
+    norms_ref[1] = penalty * jnp.sum(jnp.where(lane == 1, sums, 0.0))
+    for copy in copies:
+        copy.wait()
+
+
 def exchanged(x, axis):
     return lax.all_to_all(x, axis, 0, 0, tiled=True)
 
 
 def total_of(lines):
-    size = lax.axis_size(FEAT)
-    parts = exchanged(lines.reshape(size, -1, LANES), FEAT)
+    size = lax.axis_size(FAR)
+    parts = exchanged(lines.reshape(size, -1, LANES), FAR)
     own = jnp.sum(parts, axis=0)
-    whole = exchanged(jnp.broadcast_to(own[None], parts.shape), FEAT)
+    own = own + lax.ppermute(own, "feat_2", [(0, 1), (1, 0)])
+    whole = exchanged(jnp.broadcast_to(own[None], parts.shape), FAR)
     return whole.reshape(lines.shape)
 
 
@@ -213,27 +290,47 @@
     blocks = blocks_data[0]
     index = row_index[0]
     marks = labels.reshape(-1, LANES)
-    lines = marks.shape
     lanes, size = x.shape
+    rows = index.shape[1]
     near = lax.axis_size(NEAR)
     far = lax.axis_size(FAR)
     place = jnp.full((8, LANES), lax.axis_index("feat_2"), jnp.float32)
-    (terms,) = call(first_kernel, lines)(x, blocks, index)
+    given = (index, x, blocks, dual, consensus_old, marks)
+    terms, hots, turned, place, index, x, blocks, dual, old, marks = call(
+        first_kernel,
+        held(marks.shape),
+        held((lanes, LOW, rows), jnp.bfloat16),
+        held((lanes, size, rows), jnp.bfloat16),
+        held(place.shape),
+        *[held(each.shape, each.dtype) for each in given],
+        in_specs=[pl.BlockSpec(memory_space=pltpu.VMEM)] + [HBM] * len(given),
+        scratch_shapes=[pltpu.SemaphoreType.DMA((len(given),)), pltpu.SemaphoreType.DMA((lanes,))],
+    )(*in_vmem(place), *in_hbm(*given))
+    kept = (blocks, dual, old, marks)
     margins = total_of(terms)
-    x, terms = call(middle_kernel, x.shape, lines)(
-        *in_vmem(x, dual, consensus_old, margins, marks, blocks, index)
+    x, terms = call(middle_kernel, held(x.shape), held(marks.shape))(
+        *in_vmem(margins, hots, turned, index, x, *kept)
     )
     margins = total_of(terms)
-    x, sent = call(last_kernel, x.shape, (near, 4 * lanes, size))(
-        *in_vmem(x, dual, consensus_old, margins, marks, blocks, index)
+    x, sent = call(last_kernel, held(x.shape), held((near, 4 * lanes, size)))(
+        *in_vmem(margins, hots, turned, index, x, *kept)
     )
     came = exchanged(sent, NEAR)
-    consensus, dual_next, sums = call(consensus_kernel, x.shape, x.shape, (far, LANES))(
-        *in_vmem(came, place, x, dual)
-    )
-    sums = jnp.sum(exchanged(sums.reshape(far, 1, LANES), FAR), axis=(0, 1))
-    norms = jnp.sqrt(sums[:2]) * jnp.array([1.0, penalty], jnp.float32)
-    return (x[None], dual_next[None], consensus, norms)
+    consensus, dual, sums = call(
+        consensus_kernel, held(x.shape), held(x.shape), held((far, LANES))
+    )(*in_vmem(came, place, x, dual))
+    sums = exchanged(sums.reshape(far, 1, LANES), FAR).reshape(far, LANES)
+    whole = jax.ShapeDtypeStruct(x.shape, jnp.float32)
+    x, dual, consensus, norms = call(
+        finish_kernel,
+        whole,
+        whole,
+        whole,
+        jax.ShapeDtypeStruct((2,), jnp.float32),
+        out_specs=(HBM, HBM, HBM, pl.BlockSpec(memory_space=pltpu.SMEM)),
+        scratch_shapes=[pltpu.SemaphoreType.DMA((3,))],
+    )(*in_vmem(sums, x, dual, consensus))
+    return (x[None], dual[None], consensus, norms)
 
 
 def solution(mesh):

time: 110 us -> 106 us (0.964)
  blocking collectives: 70.4 us -> 84.9 us
  waiting for transfers between devices: 11.9 us -> 2.69 us
  starting transfers between devices: 12.7 us -> 5.64 us
  local copies, waits for them, and re-layouts: 3.03 us -> 0.03 us
    all_to_all x4 -> x6, blocking collectives: 70.4 us -> 84.9 us  [exchanged(): return lax.all_to_all(x, axis, 0, 0, tiled=True)]
    all_to_all x2 -> x0, starting transfers between devices: 12.7 us -> none  [exchanged(): return lax.all_to_all(x, axis, 0, 0, tiled=True)]
    all_to_all x2 -> x0, waiting for transfers between devices: 11.9 us -> none  [exchanged(): return lax.all_to_all(x, axis, 0, 0, tiled=True)]
    ppermute x0 -> x2, starting transfers between devices: none -> 5.64 us  [total_of(): own = own + lax.ppermute(own, 'feat_2', [(0, 1), (1, 0)])]
    ppermute x0 -> x2, waiting for transfers between devices: none -> 2.69 us  [total_of(): own = own + lax.ppermute(own, 'feat_2', [(0, 1), (1, 0)])]
    unnamed x15 -> x0, local copies, waits for them, and re-layouts: 2.46 us -> none
    pallas_call x4 -> x5, Pallas kernels: 10.9 us -> 11.3 us  [the longest x1 3.83 us: local(): call(middle_kernel, held(x.shape), held(marks.shape))]
  transfers between devices with their start and end apart: 2 -> 2, of which waited for: 2 -> 2; matrix products, arithmetic and copies ran while one was open for 2% -> 0% of each run, Pallas kernels for 0% -> 0%
where the time goes in v3:
time: 106 us; the launch traced here: 105 us
  blocking collectives  84.9 us (80%)
  Pallas kernels  11.3 us (11%)
  starting transfers between devices  5.64 us (5%)
  waiting for transfers between devices  2.69 us (3%)
    all_to_all x6, blocking collectives, exchanged(): return lax.all_to_all(x, axis, 0, 0, tiled=True)  84.9 us
    ppermute x2, starting transfers between devices, total_of(): own = own + lax.ppermute(own, 'feat_2', [(0, 1), (1, 0)])  5.64 us
    pallas_call x1, Pallas kernels, local(): call(middle_kernel, held(x.shape), held(marks.shape))  3.83 us
    pallas_call x1, Pallas kernels, local(): call(first_kernel, held(marks.shape), held((lanes, LOW, rows), jnp.bfloat...  3.45 us
    pallas_call x1, Pallas kernels, local(): call(last_kernel, held(x.shape), held((near, 4 * lanes, size)))  2.72 us
    ppermute x2, waiting for transfers between devices, total_of(): own = own + lax.ppermute(own, 'feat_2', [(0, 1), (1, 0)])  2.69 us
  transfers between devices with their start and end apart: 2, of which 2 were waited for; matrix products, arithmetic and copies ran while one was open for 0% of the time, Pallas kernels for 0%

profile of v3, /device:TPU:1, one launch (start us, length us, event | category | flops | bytes accessed | tf_op | source)
XLA Modules:
  0.0 105.3 jit_solution(16160179721887798376)
XLA Ops:
  0.6 3.4 %shard_map.93 = (f32[128,128]{1,0:T(8,128)S(1)}, bf16[4,256,512]{2,1,0:T(8,128)(2,1)S(1)}, bf16[4,256,512]{2,1,0:T(8,128)(2,1)S(1)}, f32[8,128]{1,0:T(8,128)S(1)...) custom-call(f32[8,128]{1,0:T(8,128)S(1)} %broadcast_in_dim.10.place_, ...), custom_call_target="tpu_custom_call" | custom-call | tf_op jit(solution)/shard_map/pallas_call | solution.py:299
  4.1 20.6 %all_to_all.30 = f32[32,4,128]{2,1,0:T(4,128)S(1)} all-to-all(f32[32,4,128]{2,1,0:T(4,128)S(1)} %bitcast.18), channel_id=1, replica_groups=mesh['feat_0'=8,'feat_1'=4,'feat_2'=2,'row'=2,'col'=2] {'feat_0','feat_1'}, dimensions={0} | all-to-all | bytes 131072 | tf_op jit(solution)/shard_map/all_to_all | solution.py:275
  24.8 2.8 %collective-permute-start = (f32[4,128]{1,0:T(4,128)S(1)}, f32[4,128]{1,0:T(4,128)S(1)}, u32[]{:S(2)}, u32[]{:S(2)}) collective-permute-start(f32[4,128]{1,0:T(4,128)S(1)} %reduce_sum.18), channel_id=1, source_target_pairs={{0,4},{4,0},{1,5},{5,1},{2,6},{6,2},{3,7},{7,3},{8,12},{12,8},{9,1... | collective-permute-start | bytes 6152 | tf_op jit(solution)/shard_map/ppermute | solution.py:282
  27.6 1.2 %collective-permute-done = f32[4,128]{1,0:T(4,128)S(1)} collective-permute-done((f32[4,128]{1,0:T(4,128)S(1)}, f32[4,128]{1,0:T(4,128)S(1)}, u32[]{:S(2)}, u32[]{:S(2)}) %collective-permute-start) | collective-permute-done | bytes 2080 | tf_op jit(solution)/shard_map/ppermute | solution.py:282
  28.8 11.9 %all_to_all.31 = f32[32,4,128]{2,1,0:T(4,128)S(1)} all-to-all(f32[32,4,128]{2,1,0:T(4,128)S(1)} %broadcast_in_dim.22), channel_id=1, replica_groups=mesh['feat_0'=8,'feat_1'=4,'feat_2'=2,'row'=2,'col'=2] {'feat_0','feat_1'}, dimensions={0} | all-to-all | bytes 131072 | tf_op jit(solution)/shard_map/all_to_all | solution.py:275
  40.8 3.8 %shard_map.94 = (f32[4,256]{1,0:T(4,128)S(1)}, f32[128,128]{1,0:T(8,128)S(1)}) custom-call(f32[128,128]{1,0:T(8,128)S(1)} %bitcast.16, bf16[4,256,512]{2,1,0:T(8,128)(2,1)S(1)} %get-tuple-element.26.hot_ref, bf16[4,256,512]{2,1,0:T(8,128)(2,1)S(1)} %get-tuple-element.27.turn_ref, s32[4,512]{1,0:T(4,128)S(1)} %get-tuple-element.28.idx_ref, ...), custom_call_target="tpu_custom_call" | custom-call | tf_op jit(solution)/shard_map/pallas_call | solution.py:311
  44.6 11.9 %all_to_all.32 = f32[32,4,128]{2,1,0:T(4,128)S(1)} all-to-all(f32[32,4,128]{2,1,0:T(4,128)S(1)} %bitcast.19), channel_id=1, replica_groups=mesh['feat_0'=8,'feat_1'=4,'feat_2'=2,'row'=2,'col'=2] {'feat_0','feat_1'}, dimensions={0} | all-to-all | bytes 131072 | tf_op jit(solution)/shard_map/all_to_all | solution.py:275
  56.5 2.8 %collective-permute-start.1 = (f32[4,128]{1,0:T(4,128)S(1)}, f32[4,128]{1,0:T(4,128)S(1)}, u32[]{:S(2)}, u32[]{:S(2)}) collective-permute-start(f32[4,128]{1,0:T(4,128)S(1)} %reduce_sum.19), channel_id=1, source_target_pairs={{0,4},{4,0},{1,5},{5,1},{2,6},{6,2},{3,7},{7,3},{8,12},{12,8},{9,1... | collective-permute-start | bytes 6152 | tf_op jit(solution)/shard_map/ppermute | solution.py:282
  59.4 1.5 %collective-permute-done.1 = f32[4,128]{1,0:T(4,128)S(1)} collective-permute-done((f32[4,128]{1,0:T(4,128)S(1)}, f32[4,128]{1,0:T(4,128)S(1)}, u32[]{:S(2)}, u32[]{:S(2)}) %collective-permute-start.1) | collective-permute-done | bytes 2080 | tf_op jit(solution)/shard_map/ppermute | solution.py:282
  60.9 11.8 %all_to_all.33 = f32[32,4,128]{2,1,0:T(4,128)S(1)} all-to-all(f32[32,4,128]{2,1,0:T(4,128)S(1)} %broadcast_in_dim.23), channel_id=1, replica_groups=mesh['feat_0'=8,'feat_1'=4,'feat_2'=2,'row'=2,'col'=2] {'feat_0','feat_1'}, dimensions={0} | all-to-all | bytes 131072 | tf_op jit(solution)/shard_map/all_to_all | solution.py:275
  72.7 2.7 %shard_map.95 = (f32[4,256]{1,0:T(4,128)S(1)}, f32[8,16,256]{2,1,0:T(8,128)S(1)}) custom-call(f32[128,128]{1,0:T(8,128)S(1)} %bitcast.15, bf16[4,256,512]{2,1,0:T(8,128)(2,1)S(1)} %get-tuple-element.26.hot_ref, bf16[4,256,512]{2,1,0:T(8,128)(2,1)S(1)} %get-tuple-element.27.turn_ref, s32[4,512]{1,0:T(4,128)S(1)} %get-tuple-element.28.idx_ref, ...), custom_call_target="tpu_custom_call" | custom-call | tf_op jit(solution)/shard_map/pallas_call | solution.py:315
  75.4 17.0 %all_to_all.34.came_ref = f32[8,16,256]{2,1,0:T(8,128)S(1)} all-to-all(f32[8,16,256]{2,1,0:T(8,128)S(1)} %get-tuple-element.36), channel_id=1, replica_groups=mesh['feat_0'=8,'feat_1'=4,'feat_2'=2,'row'=2,'col'=2] {'feat_2','row','..., dimensions={0} | all-to-all | bytes 262144 | tf_op jit(solution)/shard_map/all_to_all | solution.py:275
  92.4 0.1 shard_map.96
  92.5 11.6 %all_to_all.35 = f32[32,1,128]{2,1,0:T(1,128)S(1)} all-to-all(f32[32,1,128]{2,1,0:T(1,128)S(1)} %bitcast.20), channel_id=1, replica_groups=mesh['feat_0'=8,'feat_1'=4,'feat_2'=2,'row'=2,'col'=2] {'feat_0','feat_1'}, dimensions={0} | all-to-all | bytes 32768 | tf_op jit(solution)/shard_map/all_to_all | solution.py:275
  104.1 1.1 %shard_map.97 = (f32[4,256]{1,0:T(4,128)}, f32[4,256]{1,0:T(4,128)}, f32[4,256]{1,0:T(4,128)}, f32[2]{0:T(128)}) custom-call(f32[32,128]{1,0:T(8,128)S(1)} %bitcast.17, f32[4,256]{1,0:T(4,128)S(1)} %get-tuple-element.38.x_ref, f32[4,256]{1,0:T(4,128)S(1)} %get-tuple-element.40.dual_ref, f32[4,256]{1,0:T(4,128)S(1)} %get-tuple-element.41.cons_ref), custom_call_target="tpu_custom_call" | custom-call | tf_op jit(solution)/shard_map/pallas_call | solution.py:324
  (7 shorter events, 0.1 us)
Async XLA Ops:
  24.8 4.0 %collective-permute-start = (f32[4,128]{1,0:T(4,128)S(1)}, f32[4,128]{1,0:T(4,128)S(1)}, u32[]{:S(2)}, u32[]{:S(2)}) collective-permute-start(f32[4,128]{1,0:T(4,128)S(1)} %reduce_sum.18), channel_id=1, source_target_pairs={{0,4},{4,0},{1,5},{5,1},{2,6},{6,2},{3,7},{7,3},{8,12},{12,8},{9,1... | collective-permute-start | bytes 6152 | tf_op jit(solution)/shard_map/ppermute | solution.py:282
  56.5 4.3 %collective-permute-start.1 = (f32[4,128]{1,0:T(4,128)S(1)}, f32[4,128]{1,0:T(4,128)S(1)}, u32[]{:S(2)}, u32[]{:S(2)}) collective-permute-start(f32[4,128]{1,0:T(4,128)S(1)} %reduce_sum.19), channel_id=1, source_target_pairs={{0,4},{4,0},{1,5},{5,1},{2,6},{6,2},{3,7},{7,3},{8,12},{12,8},{9,1... | collective-permute-start | bytes 6152 | tf_op jit(solution)/shard_map/ppermute | solution.py:282

commit v4 on v3

--- a/solution.py
+++ b/solution.py
@@ -86,10 +86,17 @@
     return jnp.concatenate([lines[:HIGH], lines[HIGH:]], axis=1)
 
 
-def spread(rounded, turned, hot, mask, b):
-    partial = dot(rounded, turned, NN)[b : b + 1]
-    parts = [jnp.where(mask, part, 0.0) for part in three_parts(partial)]
-    return dot(jnp.concatenate(parts, axis=0).astype(jnp.bfloat16), hot, NT)
+def spread(partial, hot_ref, masks):
+    parts = three_parts(partial)
+    table = None
+    spreads = [
+        jnp.concatenate([jnp.where(mask, part[b : b + 1], 0.0) for part in parts], axis=0)
+        for b, mask in enumerate(masks)
+    ]
+    for b, spread_rows in enumerate(spreads):
+        added = dot(spread_rows.astype(jnp.bfloat16), hot_ref[b], NT)
+        table = added if table is None else table + added
+    return table
 
 
 def put(table, out_ref):
@@ -108,21 +115,23 @@
     blocks, size = x.shape
     parts = three_parts(as_table(margins)) + (as_table(labels.astype(jnp.float32)),)
     tables = jnp.concatenate(parts, axis=0).astype(jnp.bfloat16)
-    identity = identity_of(size)
-    gradients = []
-    hessians = []
-    for b, mask in enumerate(masks):
-        block = blk_ref[b]
-        found = dot(tables, hot_ref[b], NN)
-        margin = found[:HIGH] + found[HIGH : 2 * HIGH] + found[2 * HIGH : 3 * HIGH]
-        margin = jnp.sum(jnp.where(mask, margin, 0.0), axis=0, keepdims=True)
-        label = jnp.sum(jnp.where(mask, found[3 * HIGH :], 0.0), axis=0, keepdims=True)
-        prob = 1.0 / (1.0 + jnp.exp(-margin))
-        misfit = (prob - label).astype(jnp.bfloat16)
-        weight = prob * (1.0 - prob)
-        gradients.append(dot(misfit, block, NN))
-        weighted = (turn_ref[b].astype(jnp.float32) * weight).astype(jnp.bfloat16)
-        hessians.append(dot(weighted, block, NN) + penalty * identity)
+    found = [dot(tables, hot_ref[b], NN) for b in range(blocks)]
+    margin = []
+    label = []
+    for each, mask in zip(found, masks):
+        whole = each[:HIGH] + each[HIGH : 2 * HIGH] + each[2 * HIGH : 3 * HIGH]
+        margin.append(jnp.sum(jnp.where(mask, whole, 0.0), axis=0, keepdims=True))
+        label.append(jnp.sum(jnp.where(mask, each[3 * HIGH :], 0.0), axis=0, keepdims=True))
+    prob = 1.0 / (1.0 + jnp.exp(-jnp.concatenate(margin, axis=0)))
+    misfit = (prob - jnp.concatenate(label, axis=0)).astype(jnp.bfloat16)
+    weight = prob * (1.0 - prob)
+    identity = penalty * identity_of(size)
+    gradients = [dot(misfit, blk_ref[b], NN)[b : b + 1] for b in range(blocks)]
+    weighted = [
+        (turn_ref[b].astype(jnp.float32) * weight[b : b + 1]).astype(jnp.bfloat16)
+        for b in range(blocks)
+    ]
+    hessians = [dot(weighted[b], blk_ref[b], NN) + identity for b in range(blocks)]
     gradient = jnp.concatenate(gradients, axis=0) + penalty * (x - target)
     delta = jnp.zeros_like(gradient)
     residual = gradient
@@ -173,34 +182,40 @@
     for b in range(blk_ref.shape[0]):
         hot_ref[b] = low_hot(idx_ref[b : b + 1, :])
     masks = masks_of(idx_ref)
-    identity = identity_of(x_ref.shape[1]).astype(jnp.bfloat16)
     copies[1].wait()
-    rounded = x_ref[...].astype(jnp.bfloat16)
-    table = None
-    for b, mask in enumerate(masks):
-        blocks[b].wait()
-        turned = dot(identity, blk_ref[b], NT).astype(jnp.bfloat16)
-        turn_ref[b] = turned
-        added = spread(rounded, turned, hot_ref[b], mask, b)
-        table = added if table is None else table + added
-    put(table, table_ref)
+    x = x_ref[...]
+    left = jnp.concatenate([identity_of(x.shape[1])] + [x] * (16 // x.shape[0]), axis=0)
+    left = left.astype(jnp.bfloat16)
+    for copy in blocks:
+        copy.wait()
+    partial = []
+    for b in range(blk_ref.shape[0]):
+        both = dot(left, blk_ref[b], NT)
+        turn_ref[b] = both[: x.shape[1]].astype(jnp.bfloat16)
+        partial.append(both[x.shape[1] + b : x.shape[1] + b + 1])
+    put(spread(jnp.concatenate(partial, axis=0), hot_ref, masks), table_ref)
     for copy in copies[2:]:
         copy.wait()
+
+
+def summed(margin_ref):
+    lines = LANES
+    total = margin_ref[:lines]
+    for start in range(lines, margin_ref.shape[0], lines):
+        total = total + margin_ref[start : start + lines]
+    return total
 
 
 def middle_kernel(margin_ref, hot_ref, turn_ref, idx_ref, x_ref, blk_ref, dual_ref, old_ref, label_ref, x_out, out_ref):
     masks = masks_of(idx_ref)
     target = old_ref[...] - dual_ref[...]
     x = newton_step(
-        x_ref[...], target, margin_ref[...], label_ref[...], blk_ref, turn_ref, hot_ref, masks
+        x_ref[...], target, summed(margin_ref), label_ref[...], blk_ref, turn_ref, hot_ref, masks
     )
     x_out[...] = x
     rounded = x.astype(jnp.bfloat16)
-    table = None
-    for b, mask in enumerate(masks):
-        added = spread(rounded, turn_ref[b], hot_ref[b], mask, b)
-        table = added if table is None else table + added
-    put(table, out_ref)
+    partial = [dot(rounded, turn_ref[b], NN)[b : b + 1] for b in range(x.shape[0])]
+    put(spread(jnp.concatenate(partial, axis=0), hot_ref, masks), out_ref)
 
 
 def last_kernel(
@@ -210,7 +225,7 @@
     dual = dual_ref[...]
     old = old_ref[...]
     x = newton_step(
-        x_ref[...], old - dual, margin_ref[...], label_ref[...], blk_ref, turn_ref, hot_ref, masks
+        x_ref[...], old - dual, summed(margin_ref), label_ref[...], blk_ref, turn_ref, hot_ref, masks
     )
     x_out[...] = x
     sent = jnp.concatenate([x, dual, old, jnp.zeros_like(old)], axis=0)
@@ -258,16 +273,17 @@
     sums_ref[...] = jnp.broadcast_to(sums, sums_ref.shape)
 
 
-def finish_kernel(sums_ref, x_ref, dual_ref, cons_ref, x_out, dual_out, cons_out, norms_ref, sems):
+def finish_kernel(sums_ref, x_ref, dual_ref, cons_ref, x_out, dual_out, cons_out, norms_out, norms_ref, sems):
     pairs = ((x_ref, x_out), (dual_ref, dual_out), (cons_ref, cons_out))
     copies = [pltpu.make_async_copy(src, dst, sems.at[i]) for i, (src, dst) in enumerate(pairs)]
     for copy in copies:
         copy.start()
     sums = jnp.sqrt(jnp.sum(sums_ref[...], axis=0, keepdims=True))
     lane = lax.broadcasted_iota(jnp.int32, sums.shape, 1)
-    norms_ref[0] = jnp.sum(jnp.where(lane == 0, sums, 0.0))
-    norms_ref[1] = penalty * jnp.sum(jnp.where(lane == 1, sums, 0.0))
-    for copy in copies:
+    norms_ref[...] = jnp.where(lane == 1, penalty * sums, sums)[0, :2]
+    last = pltpu.make_async_copy(norms_ref, norms_out, sems.at[len(copies)])
+    last.start()
+    for copy in copies + [last]:
         copy.wait()
 
 
@@ -275,13 +291,12 @@
     return lax.all_to_all(x, axis, 0, 0, tiled=True)
 
 
-def total_of(lines):
-    size = lax.axis_size(FAR)
-    parts = exchanged(lines.reshape(size, -1, LANES), FAR)
+def tables_to_sum(lines):
+    far = lax.axis_size(FAR)
+    parts = exchanged(lines.reshape(far, -1, LANES), FAR)
     own = jnp.sum(parts, axis=0)
-    own = own + lax.ppermute(own, "feat_2", [(0, 1), (1, 0)])
-    whole = exchanged(jnp.broadcast_to(own[None], parts.shape), FAR)
-    return whole.reshape(lines.shape)
+    copies = jnp.broadcast_to(own[None], (lax.axis_size("feat_2") * far, *own.shape))
+    return exchanged(copies, ("feat_2",) + FAR).reshape(-1, LANES)
 
 
 def local(local_x, dual_var, consensus_old, blocks_data, row_index, labels):
@@ -307,11 +322,11 @@
         scratch_shapes=[pltpu.SemaphoreType.DMA((len(given),)), pltpu.SemaphoreType.DMA((lanes,))],
     )(*in_vmem(place), *in_hbm(*given))
     kept = (blocks, dual, old, marks)
-    margins = total_of(terms)
+    margins = tables_to_sum(terms)
     x, terms = call(middle_kernel, held(x.shape), held(marks.shape))(
         *in_vmem(margins, hots, turned, index, x, *kept)
     )
-    margins = total_of(terms)
+    margins = tables_to_sum(terms)
     x, sent = call(last_kernel, held(x.shape), held((near, 4 * lanes, size)))(
         *in_vmem(margins, hots, turned, index, x, *kept)
     )
@@ -327,8 +342,8 @@
         whole,
         whole,
         jax.ShapeDtypeStruct((2,), jnp.float32),
-        out_specs=(HBM, HBM, HBM, pl.BlockSpec(memory_space=pltpu.SMEM)),
-        scratch_shapes=[pltpu.SemaphoreType.DMA((3,))],
+        out_specs=(HBM, HBM, HBM, HBM),
+        scratch_shapes=[pltpu.VMEM((2,), jnp.float32), pltpu.SemaphoreType.DMA((4,))],
     )(*in_vmem(sums, x, dual, consensus))
     return (x[None], dual[None], consensus, norms)
 

time: 106 us -> 101 us (0.953)
  starting transfers between devices: 5.64 us -> 0 us
  blocking collectives: 84.9 us -> 90.5 us
  waiting for transfers between devices: 2.69 us -> 0 us
  Pallas kernels: 11.3 us -> 9.01 us
    ppermute x2 -> x0, starting transfers between devices: 5.64 us -> none  [total_of(): own = own + lax.ppermute(own, 'feat_2', [(0, 1), (1, 0)])]
    all_to_all x6, blocking collectives: 84.9 us -> 90.5 us  [exchanged(): return lax.all_to_all(x, axis, 0, 0, tiled=True)]
    ppermute x2 -> x0, waiting for transfers between devices: 2.69 us -> none  [total_of(): own = own + lax.ppermute(own, 'feat_2', [(0, 1), (1, 0)])]
  transfers between devices with their start and end apart: 2 -> 0, of which waited for: 2 -> 0; matrix products, arithmetic and copies ran while one was open for 0% -> 0% of each run, Pallas kernels for 0% -> 0%
where the time goes in v4:
time: 101 us; the launch traced here: 100 us
  blocking collectives  90.5 us (90%)
  Pallas kernels  9.01 us (9%)
    all_to_all x6, blocking collectives, exchanged(): return lax.all_to_all(x, axis, 0, 0, tiled=True)  90.5 us
    pallas_call x1, Pallas kernels, local(): call(middle_kernel, held(x.shape), held(marks.shape))  3.48 us
    pallas_call x1, Pallas kernels, local(): call(first_kernel, held(marks.shape), held((lanes, LOW, rows), jnp.bfloat...  2.6 us
    pallas_call x1, Pallas kernels, local(): call(last_kernel, held(x.shape), held((near, 4 * lanes, size)))  2.18 us

profile of v4, /device:TPU:1, one launch (start us, length us, event | category | flops | bytes accessed | tf_op | source)
XLA Modules:
  0.0 100.3 jit_solution(12168729160177752334)
XLA Ops:
  0.6 2.6 %shard_map.93 = (f32[128,128]{1,0:T(8,128)S(1)}, bf16[4,256,512]{2,1,0:T(8,128)(2,1)S(1)}, bf16[4,256,512]{2,1,0:T(8,128)(2,1)S(1)}, f32[8,128]{1,0:T(8,128)S(1)...) custom-call(f32[8,128]{1,0:T(8,128)S(1)} %broadcast_in_dim.10.place_, ...), custom_call_target="tpu_custom_call" | custom-call | tf_op jit(solution)/shard_map/pallas_call | solution.py:314
  3.3 20.6 %all_to_all.30 = f32[32,4,128]{2,1,0:T(4,128)S(1)} all-to-all(f32[32,4,128]{2,1,0:T(4,128)S(1)} %bitcast.18), channel_id=1, replica_groups=mesh['feat_0'=8,'feat_1'=4,'feat_2'=2,'row'=2,'col'=2] {'feat_0','feat_1'}, dimensions={0} | all-to-all | bytes 131072 | tf_op jit(solution)/shard_map/all_to_all | solution.py:291
  24.0 17.7 %all_to_all.31 = f32[64,4,128]{2,1,0:T(4,128)S(1)} all-to-all(f32[64,4,128]{2,1,0:T(4,128)S(1)} %broadcast_in_dim.22), channel_id=1, replica_groups=mesh['feat_0'=8,'feat_1'=4,'feat_2'=2,'row'=2,'col'=2] {'feat_2','feat_0..., dimensions={0} | all-to-all | bytes 262144 | tf_op jit(solution)/shard_map/all_to_all | solution.py:291
  41.6 3.5 %shard_map.94 = (f32[4,256]{1,0:T(4,128)S(1)}, f32[128,128]{1,0:T(8,128)S(1)}) custom-call(f32[256,128]{1,0:T(8,128)S(1)} %bitcast.16, bf16[4,256,512]{2,1,0:T(8,128)(2,1)S(1)} %get-tuple-element.26.hot_ref, bf16[4,256,512]{2,1,0:T(8,128)(2,1)S(1)} %get-tuple-element.27.turn_ref, s32[4,512]{1,0:T(4,128)S(1)} %get-tuple-element.28.idx_ref, ...), custom_call_target="tpu_custom_call" | custom-call | tf_op jit(solution)/shard_map/pallas_call | solution.py:326
  45.1 12.1 %all_to_all.32 = f32[32,4,128]{2,1,0:T(4,128)S(1)} all-to-all(f32[32,4,128]{2,1,0:T(4,128)S(1)} %bitcast.19), channel_id=1, replica_groups=mesh['feat_0'=8,'feat_1'=4,'feat_2'=2,'row'=2,'col'=2] {'feat_0','feat_1'}, dimensions={0} | all-to-all | bytes 131072 | tf_op jit(solution)/shard_map/all_to_all | solution.py:291
  57.3 15.3 %all_to_all.33 = f32[64,4,128]{2,1,0:T(4,128)S(1)} all-to-all(f32[64,4,128]{2,1,0:T(4,128)S(1)} %broadcast_in_dim.23), channel_id=1, replica_groups=mesh['feat_0'=8,'feat_1'=4,'feat_2'=2,'row'=2,'col'=2] {'feat_2','feat_0..., dimensions={0} | all-to-all | bytes 262144 | tf_op jit(solution)/shard_map/all_to_all | solution.py:291
  72.6 2.2 %shard_map.95 = (f32[4,256]{1,0:T(4,128)S(1)}, f32[8,16,256]{2,1,0:T(8,128)S(1)}) custom-call(f32[256,128]{1,0:T(8,128)S(1)} %bitcast.15, bf16[4,256,512]{2,1,0:T(8,128)(2,1)S(1)} %get-tuple-element.26.hot_ref, bf16[4,256,512]{2,1,0:T(8,128)(2,1)S(1)} %get-tuple-element.27.turn_ref, s32[4,512]{1,0:T(4,128)S(1)} %get-tuple-element.28.idx_ref, ...), custom_call_target="tpu_custom_call" | custom-call | tf_op jit(solution)/shard_map/pallas_call | solution.py:330
  74.8 13.2 %all_to_all.34.came_ref = f32[8,16,256]{2,1,0:T(8,128)S(1)} all-to-all(f32[8,16,256]{2,1,0:T(8,128)S(1)} %get-tuple-element.36), channel_id=1, replica_groups=mesh['feat_0'=8,'feat_1'=4,'feat_2'=2,'row'=2,'col'=2] {'feat_2','row','..., dimensions={0} | all-to-all | bytes 262144 | tf_op jit(solution)/shard_map/all_to_all | solution.py:291
  88.0 0.1 shard_map.96
  88.1 11.6 %all_to_all.35 = f32[32,1,128]{2,1,0:T(1,128)S(1)} all-to-all(f32[32,1,128]{2,1,0:T(1,128)S(1)} %bitcast.20), channel_id=1, replica_groups=mesh['feat_0'=8,'feat_1'=4,'feat_2'=2,'row'=2,'col'=2] {'feat_0','feat_1'}, dimensions={0} | all-to-all | bytes 32768 | tf_op jit(solution)/shard_map/all_to_all | solution.py:291
  99.7 0.6 shard_map.97
  (5 shorter events, 0.1 us)

commit v5 on v4

--- a/solution.py
+++ b/solution.py
@@ -105,25 +105,36 @@
     out_ref[HIGH:, :] = table[:, LANES:]
 
 
+def picked(found, masks):
+    rows = [
+        jnp.sum(jnp.where(mask, each, 0.0), axis=0, keepdims=True)
+        for each, mask in zip(found, masks)
+    ]
+    return jnp.concatenate(rows, axis=0)
+
+
 def identity_of(size):
     rows = lax.broadcasted_iota(jnp.int32, (size, size), 0)
     cols = lax.broadcasted_iota(jnp.int32, (size, size), 1)
     return jnp.where(rows == cols, 1.0, 0.0)
 
 
+def as_column(line):
+    size = line.shape[1]
+    pieces = [
+        jnp.transpose(jnp.broadcast_to(line[:, start : start + LANES], (LANES, LANES)))
+        for start in range(0, size, LANES)
+    ]
+    return jnp.concatenate([jnp.concatenate(pieces, axis=0)] * (size // LANES), axis=1)
+
+
 def newton_step(x, target, margins, labels, blk_ref, turn_ref, hot_ref, masks):
     blocks, size = x.shape
-    parts = three_parts(as_table(margins)) + (as_table(labels.astype(jnp.float32)),)
-    tables = jnp.concatenate(parts, axis=0).astype(jnp.bfloat16)
+    tables = jnp.concatenate(three_parts(as_table(margins)), axis=0).astype(jnp.bfloat16)
     found = [dot(tables, hot_ref[b], NN) for b in range(blocks)]
-    margin = []
-    label = []
-    for each, mask in zip(found, masks):
-        whole = each[:HIGH] + each[HIGH : 2 * HIGH] + each[2 * HIGH : 3 * HIGH]
-        margin.append(jnp.sum(jnp.where(mask, whole, 0.0), axis=0, keepdims=True))
-        label.append(jnp.sum(jnp.where(mask, each[3 * HIGH :], 0.0), axis=0, keepdims=True))
-    prob = 1.0 / (1.0 + jnp.exp(-jnp.concatenate(margin, axis=0)))
-    misfit = (prob - jnp.concatenate(label, axis=0)).astype(jnp.bfloat16)
+    found = [each[:HIGH] + each[HIGH : 2 * HIGH] + each[2 * HIGH :] for each in found]
+    prob = 1.0 / (1.0 + jnp.exp(-picked(found, masks)))
+    misfit = (prob - labels).astype(jnp.bfloat16)
     weight = prob * (1.0 - prob)
     identity = penalty * identity_of(size)
     gradients = [dot(misfit, blk_ref[b], NN)[b : b + 1] for b in range(blocks)]
@@ -138,10 +149,9 @@
     direction = gradient
     power = jnp.sum(residual * residual, axis=1, keepdims=True)
     for cg_step in range(CG_STEPS):
-        column = jnp.transpose(jnp.concatenate([direction, direction], axis=0))
         image = jnp.concatenate(
             [
-                jnp.sum(hessians[b] * column[:, b : b + 1], axis=0, keepdims=True)
+                jnp.sum(hessians[b] * as_column(direction[b : b + 1]), axis=0, keepdims=True)
                 for b in range(blocks)
             ],
             axis=0,
@@ -160,7 +170,9 @@
 
 
 def first_kernel(place_ref, *refs):
-    given, (table_ref, hot_ref, turn_ref, place_out, *kept), (sems, block_sems) = refs[:6], refs[6:-2], refs[-2:]
+    given, (table_ref, hot_ref, turn_ref, place_out, label_ref, *kept), scratch = refs[:6], refs[6:-3], refs[-3:]
+    marks_ref, sems, block_sems = scratch
+    kept = (*kept, marks_ref)
     (idx_in, x_in, blk_in, *_), (idx_ref, x_ref, blk_ref, *_) = given, kept
     copies = [
         pltpu.make_async_copy(src, dst, sems.at[i])
@@ -171,17 +183,17 @@
         pltpu.make_async_copy(blk_in.at[b], blk_ref.at[b], block_sems.at[b])
         for b in range(blk_ref.shape[0])
     ]
-    copies[0].start()
-    copies[1].start()
-    for copy in blocks:
-        copy.start()
-    for copy in copies[2:]:
+    for copy in (copies[0], copies[1], copies[-1], *blocks, *copies[2:-1]):
         copy.start()
     place_out[...] = place_ref[...]
     copies[0].wait()
     for b in range(blk_ref.shape[0]):
         hot_ref[b] = low_hot(idx_ref[b : b + 1, :])
     masks = masks_of(idx_ref)
+    copies[-1].wait()
+    marks = as_table(marks_ref[...].astype(jnp.float32)).astype(jnp.bfloat16)
+    found = [dot(marks, hot_ref[b], NN) for b in range(blk_ref.shape[0])]
+    label_ref[...] = picked(found, masks)
     copies[1].wait()
     x = x_ref[...]
     left = jnp.concatenate([identity_of(x.shape[1])] + [x] * (16 // x.shape[0]), axis=0)
@@ -194,7 +206,7 @@
         turn_ref[b] = both[: x.shape[1]].astype(jnp.bfloat16)
         partial.append(both[x.shape[1] + b : x.shape[1] + b + 1])
     put(spread(jnp.concatenate(partial, axis=0), hot_ref, masks), table_ref)
-    for copy in copies[2:]:
+    for copy in copies[2:-1]:
         copy.wait()
 
 
@@ -228,9 +240,9 @@
         x_ref[...], old - dual, summed(margin_ref), label_ref[...], blk_ref, turn_ref, hot_ref, masks
     )
     x_out[...] = x
-    sent = jnp.concatenate([x, dual, old, jnp.zeros_like(old)], axis=0)
     for peer in range(sent_ref.shape[0]):
-        sent_ref[peer] = sent
+        for i, sent in enumerate((x, dual, old)):
+            sent_ref[peer, i] = sent
 
 
 def full_sum(values):
@@ -238,17 +250,17 @@
 
 
 def consensus_kernel(came_ref, place_ref, x_ref, dual_ref, cons_ref, dual_out, sums_ref):
-    blocks = x_ref.shape[0]
     groups = came_ref.shape[0] // SHARDS
     primal = change = None
     found = []
     for group in range(groups):
-        came = [came_ref[group * SHARDS + i] for i in range(SHARDS)]
-        solved = [each[:blocks] for each in came]
-        old = came[0][2 * blocks : 3 * blocks]
-        total = solved[0] + came[0][blocks : 2 * blocks]
-        for i in range(1, SHARDS):
-            total = total + (solved[i] + came[i][blocks : 2 * blocks])
+        peers = range(group * SHARDS, (group + 1) * SHARDS)
+        solved = [came_ref[i, 0] for i in peers]
+        both = [came_ref[i, 0] + came_ref[i, 1] for i in peers]
+        old = came_ref[group * SHARDS, 2]
+        total = both[0]
+        for each in both[1:]:
+            total = total + each
         averaged = total / float(SHARDS)
         cut = jnp.maximum(jnp.abs(averaged) - threshold, 0.0)
         consensus = jnp.where(averaged < 0.0, -cut, cut)
@@ -311,23 +323,28 @@
     far = lax.axis_size(FAR)
     place = jnp.full((8, LANES), lax.axis_index("feat_2"), jnp.float32)
     given = (index, x, blocks, dual, consensus_old, marks)
-    terms, hots, turned, place, index, x, blocks, dual, old, marks = call(
+    terms, hots, turned, place, label, index, x, blocks, dual, old = call(
         first_kernel,
         held(marks.shape),
         held((lanes, LOW, rows), jnp.bfloat16),
         held((lanes, size, rows), jnp.bfloat16),
         held(place.shape),
-        *[held(each.shape, each.dtype) for each in given],
+        held(index.shape),
+        *[held(each.shape, each.dtype) for each in given[:-1]],
         in_specs=[pl.BlockSpec(memory_space=pltpu.VMEM)] + [HBM] * len(given),
-        scratch_shapes=[pltpu.SemaphoreType.DMA((len(given),)), pltpu.SemaphoreType.DMA((lanes,))],
+        scratch_shapes=[
+            pltpu.VMEM(marks.shape, marks.dtype),
+            pltpu.SemaphoreType.DMA((len(given),)),
+            pltpu.SemaphoreType.DMA((lanes,)),
+        ],
     )(*in_vmem(place), *in_hbm(*given))
-    kept = (blocks, dual, old, marks)
+    kept = (blocks, dual, old, label)
     margins = tables_to_sum(terms)
     x, terms = call(middle_kernel, held(x.shape), held(marks.shape))(
         *in_vmem(margins, hots, turned, index, x, *kept)
     )
     margins = tables_to_sum(terms)
-    x, sent = call(last_kernel, held(x.shape), held((near, 4 * lanes, size)))(
+    x, sent = call(last_kernel, held(x.shape), held((near, 3, lanes, size)))(
         *in_vmem(margins, hots, turned, index, x, *kept)
     )
     came = exchanged(sent, NEAR)

time: 101 us -> 99.7 us (0.987)
  no operation moved by 1% of the time
where the time goes in v5:
time: 99.7 us; the launch traced here: 99.4 us
  blocking collectives  90.3 us (91%)
  Pallas kernels  8.29 us (8%)
    all_to_all x6, blocking collectives, exchanged(): return lax.all_to_all(x, axis, 0, 0, tiled=True)  90.3 us
    pallas_call x1, Pallas kernels, local(): call(middle_kernel, held(x.shape), held(marks.shape))  2.92 us
    pallas_call x1, Pallas kernels, local(): call(first_kernel, held(marks.shape), held((lanes, LOW, rows), jnp.bfloat...  2.81 us

profile of v5, /device:TPU:1, one launch (start us, length us, event | category | flops | bytes accessed | tf_op | source)
XLA Modules:
  0.0 99.4 jit_solution(10657056934676168075)
XLA Ops:
  0.6 2.8 %shard_map.93 = (f32[128,128]{1,0:T(8,128)S(1)}, bf16[4,256,512]{2,1,0:T(8,128)(2,1)S(1)}, bf16[4,256,512]{2,1,0:T(8,128)(2,1)S(1)}, f32[8,128]{1,0:T(8,128)S(1)...) custom-call(f32[8,128]{1,0:T(8,128)S(1)} %broadcast_in_dim.10.place_, ...), custom_call_target="tpu_custom_call" | custom-call | tf_op jit(solution)/shard_map/pallas_call | solution.py:326
  3.5 20.6 %all_to_all.30 = f32[32,4,128]{2,1,0:T(4,128)S(1)} all-to-all(f32[32,4,128]{2,1,0:T(4,128)S(1)} %bitcast.18), channel_id=1, replica_groups=mesh['feat_0'=8,'feat_1'=4,'feat_2'=2,'row'=2,'col'=2] {'feat_0','feat_1'}, dimensions={0} | all-to-all | bytes 131072 | tf_op jit(solution)/shard_map/all_to_all | solution.py:303
  24.2 17.7 %all_to_all.31 = f32[64,4,128]{2,1,0:T(4,128)S(1)} all-to-all(f32[64,4,128]{2,1,0:T(4,128)S(1)} %broadcast_in_dim.22), channel_id=1, replica_groups=mesh['feat_0'=8,'feat_1'=4,'feat_2'=2,'row'=2,'col'=2] {'feat_2','feat_0..., dimensions={0} | all-to-all | bytes 262144 | tf_op jit(solution)/shard_map/all_to_all | solution.py:303
  41.8 2.9 %shard_map.94 = (f32[4,256]{1,0:T(4,128)S(1)}, f32[128,128]{1,0:T(8,128)S(1)}) custom-call(f32[256,128]{1,0:T(8,128)S(1)} %bitcast.16, bf16[4,256,512]{2,1,0:T(8,128)(2,1)S(1)} %get-tuple-element.26.hot_ref, bf16[4,256,512]{2,1,0:T(8,128)(2,1)S(1)} %get-tuple-element.27.turn_ref, s32[4,512]{1,0:T(4,128)S(1)} %get-tuple-element.28.idx_ref, ...), custom_call_target="tpu_custom_call" | custom-call | tf_op jit(solution)/shard_map/pallas_call | solution.py:343
  44.8 12.1 %all_to_all.32 = f32[32,4,128]{2,1,0:T(4,128)S(1)} all-to-all(f32[32,4,128]{2,1,0:T(4,128)S(1)} %bitcast.19), channel_id=1, replica_groups=mesh['feat_0'=8,'feat_1'=4,'feat_2'=2,'row'=2,'col'=2] {'feat_0','feat_1'}, dimensions={0} | all-to-all | bytes 131072 | tf_op jit(solution)/shard_map/all_to_all | solution.py:303
  57.0 15.3 %all_to_all.33 = f32[64,4,128]{2,1,0:T(4,128)S(1)} all-to-all(f32[64,4,128]{2,1,0:T(4,128)S(1)} %broadcast_in_dim.23), channel_id=1, replica_groups=mesh['feat_0'=8,'feat_1'=4,'feat_2'=2,'row'=2,'col'=2] {'feat_2','feat_0..., dimensions={0} | all-to-all | bytes 262144 | tf_op jit(solution)/shard_map/all_to_all | solution.py:303
  72.2 1.8 %shard_map.95 = (f32[4,256]{1,0:T(4,128)S(1)}, f32[8,3,4,256]{3,2,1,0:T(4,128)S(1)}) custom-call(f32[256,128]{1,0:T(8,128)S(1)} %bitcast.15, bf16[4,256,512]{2,1,0:T(8,128)(2,1)S(1)} %get-tuple-element.26.hot_ref, bf16[4,256,512]{2,1,0:T(8,128)(2,1)S(1)} %get-tuple-element.27.turn_ref, s32[4,512]{1,0:T(4,128)S(1)} %get-tuple-element.28.idx_ref, ...), custom_call_target="tpu_custom_call" | custom-call | tf_op jit(solution)/shard_map/pallas_call | solution.py:347
  74.0 12.9 %all_to_all.34.came_ref = f32[8,3,4,256]{3,2,1,0:T(4,128)S(1)} all-to-all(f32[8,3,4,256]{3,2,1,0:T(4,128)S(1)} %get-tuple-element.36), channel_id=1, replica_groups=mesh['feat_0'=8,'feat_1'=4,'feat_2'=2,'row'=2,'col'=2] {'feat_2','row','..., dimensions={0} | all-to-all | bytes 196608 | tf_op jit(solution)/shard_map/all_to_all | solution.py:303
  87.0 0.1 shard_map.96
  87.1 11.6 %all_to_all.35 = f32[32,1,128]{2,1,0:T(1,128)S(1)} all-to-all(f32[32,1,128]{2,1,0:T(1,128)S(1)} %bitcast.20), channel_id=1, replica_groups=mesh['feat_0'=8,'feat_1'=4,'feat_2'=2,'row'=2,'col'=2] {'feat_0','feat_1'}, dimensions={0} | all-to-all | bytes 32768 | tf_op jit(solution)/shard_map/all_to_all | solution.py:303
  98.7 0.6 shard_map.97
  (5 shorter events, 0.1 us)

commit v6 on v5

--- a/solution.py
+++ b/solution.py
@@ -86,7 +86,7 @@
     return jnp.concatenate([lines[:HIGH], lines[HIGH:]], axis=1)
 
 
-def spread(partial, hot_ref, masks):
+def spread(partial, hot_ref, masks, dims):
     parts = three_parts(partial)
     table = None
     spreads = [
@@ -94,7 +94,7 @@
         for b, mask in enumerate(masks)
     ]
     for b, spread_rows in enumerate(spreads):
-        added = dot(spread_rows.astype(jnp.bfloat16), hot_ref[b], NT)
+        added = dot(spread_rows.astype(jnp.bfloat16), hot_ref[b], dims)
         table = added if table is None else table + added
     return table
 
@@ -195,17 +195,15 @@
     found = [dot(marks, hot_ref[b], NN) for b in range(blk_ref.shape[0])]
     label_ref[...] = picked(found, masks)
     copies[1].wait()
-    x = x_ref[...]
-    left = jnp.concatenate([identity_of(x.shape[1])] + [x] * (16 // x.shape[0]), axis=0)
-    left = left.astype(jnp.bfloat16)
+    rounded = x_ref[...].astype(jnp.bfloat16)
     for copy in blocks:
         copy.wait()
     partial = []
     for b in range(blk_ref.shape[0]):
-        both = dot(left, blk_ref[b], NT)
-        turn_ref[b] = both[: x.shape[1]].astype(jnp.bfloat16)
-        partial.append(both[x.shape[1] + b : x.shape[1] + b + 1])
-    put(spread(jnp.concatenate(partial, axis=0), hot_ref, masks), table_ref)
+        turned = jnp.transpose(blk_ref[b])
+        turn_ref[b] = turned
+        partial.append(dot(rounded, turned, NN)[b : b + 1])
+    put(spread(jnp.concatenate(partial, axis=0), hot_ref, masks, NT), table_ref)
     for copy in copies[2:-1]:
         copy.wait()
 
@@ -218,8 +216,10 @@
     return total
 
 
-def middle_kernel(margin_ref, hot_ref, turn_ref, idx_ref, x_ref, blk_ref, dual_ref, old_ref, label_ref, x_out, out_ref):
+def middle_kernel(margin_ref, hot_ref, turn_ref, idx_ref, x_ref, blk_ref, dual_ref, old_ref, label_ref, x_out, out_ref, stood_ref):
     masks = masks_of(idx_ref)
+    for b in range(x_ref.shape[0]):
+        stood_ref[b] = jnp.transpose(hot_ref[b])
     target = old_ref[...] - dual_ref[...]
     x = newton_step(
         x_ref[...], target, summed(margin_ref), label_ref[...], blk_ref, turn_ref, hot_ref, masks
@@ -227,7 +227,7 @@
     x_out[...] = x
     rounded = x.astype(jnp.bfloat16)
     partial = [dot(rounded, turn_ref[b], NN)[b : b + 1] for b in range(x.shape[0])]
-    put(spread(jnp.concatenate(partial, axis=0), hot_ref, masks), out_ref)
+    put(spread(jnp.concatenate(partial, axis=0), stood_ref, masks, NN), out_ref)
 
 
 def last_kernel(
@@ -340,7 +340,12 @@
     )(*in_vmem(place), *in_hbm(*given))
     kept = (blocks, dual, old, label)
     margins = tables_to_sum(terms)
-    x, terms = call(middle_kernel, held(x.shape), held(marks.shape))(
+    x, terms = call(
+        middle_kernel,
+        held(x.shape),
+        held(marks.shape),
+        scratch_shapes=[pltpu.VMEM((lanes, rows, LOW), jnp.bfloat16)],
+    )(
         *in_vmem(margins, hots, turned, index, x, *kept)
     )
     margins = tables_to_sum(terms)

time: 99.7 us -> 99.1 us (level)
  no operation moved by 1% of the time
where the time goes in v6:
time: 99.1 us; the launch traced here: 98.8 us
  blocking collectives  90.3 us (91%)
  Pallas kernels  7.68 us (8%)
    all_to_all x6, blocking collectives, exchanged(): return lax.all_to_all(x, axis, 0, 0, tiled=True)  90.3 us
    pallas_call x1, Pallas kernels, local(): call(middle_kernel, held(x.shape), held(marks.shape), scratch_shapes=[plt...  2.75 us
    pallas_call x1, Pallas kernels, local(): call(first_kernel, held(marks.shape), held((lanes, LOW, rows), jnp.bfloat...  2.36 us

profile of v6, /device:TPU:1, one launch (start us, length us, event | category | flops | bytes accessed | tf_op | source)
XLA Modules:
  0.0 98.8 jit_solution(5603359445828537411)
XLA Ops:
  0.6 2.4 %shard_map.93 = (f32[128,128]{1,0:T(8,128)S(1)}, bf16[4,256,512]{2,1,0:T(8,128)(2,1)S(1)}, bf16[4,256,512]{2,1,0:T(8,128)(2,1)S(1)}, f32[8,128]{1,0:T(8,128)S(1)...) custom-call(f32[8,128]{1,0:T(8,128)S(1)} %broadcast_in_dim.10.place_, ...), custom_call_target="tpu_custom_call" | custom-call | tf_op jit(solution)/shard_map/pallas_call | solution.py:326
  3.0 20.6 %all_to_all.30 = f32[32,4,128]{2,1,0:T(4,128)S(1)} all-to-all(f32[32,4,128]{2,1,0:T(4,128)S(1)} %bitcast.18), channel_id=1, replica_groups=mesh['feat_0'=8,'feat_1'=4,'feat_2'=2,'row'=2,'col'=2] {'feat_0','feat_1'}, dimensions={0} | all-to-all | bytes 131072 | tf_op jit(solution)/shard_map/all_to_all | solution.py:303
  23.7 17.7 %all_to_all.31 = f32[64,4,128]{2,1,0:T(4,128)S(1)} all-to-all(f32[64,4,128]{2,1,0:T(4,128)S(1)} %broadcast_in_dim.22), channel_id=1, replica_groups=mesh['feat_0'=8,'feat_1'=4,'feat_2'=2,'row'=2,'col'=2] {'feat_2','feat_0..., dimensions={0} | all-to-all | bytes 262144 | tf_op jit(solution)/shard_map/all_to_all | solution.py:303
  41.4 2.7 %shard_map.94 = (f32[4,256]{1,0:T(4,128)S(1)}, f32[128,128]{1,0:T(8,128)S(1)}) custom-call(f32[256,128]{1,0:T(8,128)S(1)} %bitcast.16, bf16[4,256,512]{2,1,0:T(8,128)(2,1)S(1)} %get-tuple-element.26.hot_ref, bf16[4,256,512]{2,1,0:T(8,128)(2,1)S(1)} %get-tuple-element.27.turn_ref, s32[4,512]{1,0:T(4,128)S(1)} %get-tuple-element.28.idx_ref, ...), custom_call_target="tpu_custom_call" | custom-call | tf_op jit(solution)/shard_map/pallas_call | solution.py:343
  44.1 12.1 %all_to_all.32 = f32[32,4,128]{2,1,0:T(4,128)S(1)} all-to-all(f32[32,4,128]{2,1,0:T(4,128)S(1)} %bitcast.19), channel_id=1, replica_groups=mesh['feat_0'=8,'feat_1'=4,'feat_2'=2,'row'=2,'col'=2] {'feat_0','feat_1'}, dimensions={0} | all-to-all | bytes 131072 | tf_op jit(solution)/shard_map/all_to_all | solution.py:303
  56.3 15.3 %all_to_all.33 = f32[64,4,128]{2,1,0:T(4,128)S(1)} all-to-all(f32[64,4,128]{2,1,0:T(4,128)S(1)} %broadcast_in_dim.23), channel_id=1, replica_groups=mesh['feat_0'=8,'feat_1'=4,'feat_2'=2,'row'=2,'col'=2] {'feat_2','feat_0..., dimensions={0} | all-to-all | bytes 262144 | tf_op jit(solution)/shard_map/all_to_all | solution.py:303
  71.6 1.8 %shard_map.95 = (f32[4,256]{1,0:T(4,128)S(1)}, f32[8,3,4,256]{3,2,1,0:T(4,128)S(1)}) custom-call(f32[256,128]{1,0:T(8,128)S(1)} %bitcast.15, bf16[4,256,512]{2,1,0:T(8,128)(2,1)S(1)} %get-tuple-element.26.hot_ref, bf16[4,256,512]{2,1,0:T(8,128)(2,1)S(1)} %get-tuple-element.27.turn_ref, s32[4,512]{1,0:T(4,128)S(1)} %get-tuple-element.28.idx_ref, ...), custom_call_target="tpu_custom_call" | custom-call | tf_op jit(solution)/shard_map/pallas_call | solution.py:352
  73.4 12.9 %all_to_all.34.came_ref = f32[8,3,4,256]{3,2,1,0:T(4,128)S(1)} all-to-all(f32[8,3,4,256]{3,2,1,0:T(4,128)S(1)} %get-tuple-element.36), channel_id=1, replica_groups=mesh['feat_0'=8,'feat_1'=4,'feat_2'=2,'row'=2,'col'=2] {'feat_2','row','..., dimensions={0} | all-to-all | bytes 196608 | tf_op jit(solution)/shard_map/all_to_all | solution.py:303
  86.3 0.1 shard_map.96
  86.5 11.7 %all_to_all.35 = f32[32,1,128]{2,1,0:T(1,128)S(1)} all-to-all(f32[32,1,128]{2,1,0:T(1,128)S(1)} %bitcast.20), channel_id=1, replica_groups=mesh['feat_0'=8,'feat_1'=4,'feat_2'=2,'row'=2,'col'=2] {'feat_0','feat_1'}, dimensions={0} | all-to-all | bytes 32768 | tf_op jit(solution)/shard_map/all_to_all | solution.py:303
  98.1 0.6 shard_map.97
  (5 shorter events, 0.1 us)

commit v7 on v6

--- a/solution.py
+++ b/solution.py
@@ -7,10 +7,11 @@
 from jax.sharding import PartitionSpec as P
 
 CG_STEPS = 3
-FEAT = ("feat_0", "feat_1", "feat_2")
+FEAT = ("z", "y_hi", "y_lo", "x_hi")
 SHARD = ("row", "col")
-NEAR = ("feat_2", "row", "col")
-FAR = ("feat_0", "feat_1")
+NEAR = ("x_hi", "row", "col")
+FAR = ("z", "y_hi", "y_lo")
+ACROSS = ("x_hi", "z", "y_lo")
 LANES = 128
 HIGH = 64
 LOW = 256
@@ -101,8 +102,11 @@
 
 def put(table, out_ref):
     table = table[:HIGH] + table[HIGH : 2 * HIGH] + table[2 * HIGH :]
-    out_ref[:HIGH, :] = table[:, :LANES]
-    out_ref[HIGH:, :] = table[:, LANES:]
+    table = jnp.concatenate([table[:, :LANES], table[:, LANES:]], axis=0)
+    parts, copies, lines, _ = out_ref.shape
+    for part in range(parts):
+        for copy in range(copies):
+            out_ref[part, copy] = table[part * lines : (part + 1) * lines]
 
 
 def picked(found, masks):
@@ -303,12 +307,11 @@
     return lax.all_to_all(x, axis, 0, 0, tiled=True)
 
 
-def tables_to_sum(lines):
-    far = lax.axis_size(FAR)
-    parts = exchanged(lines.reshape(far, -1, LANES), FAR)
-    own = jnp.sum(parts, axis=0)
-    copies = jnp.broadcast_to(own[None], (lax.axis_size("feat_2") * far, *own.shape))
-    return exchanged(copies, ("feat_2",) + FAR).reshape(-1, LANES)
+def tables_to_sum(terms):
+    pieces = terms.reshape(lax.axis_size(FAR), -1, LANES)
+    own = jnp.sum(exchanged(pieces, FAR), axis=0)
+    copies = jnp.broadcast_to(own[None], (lax.axis_size(ACROSS), *own.shape))
+    return exchanged(copies, ACROSS).reshape(-1, LANES)
 
 
 def local(local_x, dual_var, consensus_old, blocks_data, row_index, labels):
@@ -321,11 +324,13 @@
     rows = index.shape[1]
     near = lax.axis_size(NEAR)
     far = lax.axis_size(FAR)
-    place = jnp.full((8, LANES), lax.axis_index("feat_2"), jnp.float32)
+    place = jnp.full((8, LANES), lax.axis_index("x_hi"), jnp.float32)
+    zs = lax.axis_size("z")
+    spread_out = held((zs, lax.axis_size("y_hi"), marks.shape[0] // zs, LANES))
     given = (index, x, blocks, dual, consensus_old, marks)
     terms, hots, turned, place, label, index, x, blocks, dual, old = call(
         first_kernel,
-        held(marks.shape),
+        spread_out,
         held((lanes, LOW, rows), jnp.bfloat16),
         held((lanes, size, rows), jnp.bfloat16),
         held(place.shape),
@@ -343,7 +348,7 @@
     x, terms = call(
         middle_kernel,
         held(x.shape),
-        held(marks.shape),
+        spread_out,
         scratch_shapes=[pltpu.VMEM((lanes, rows, LOW), jnp.bfloat16)],
     )(
         *in_vmem(margins, hots, turned, index, x, *kept)
@@ -371,10 +376,7 @@
 
 
 def solution(mesh):
-    if mesh.shape["feat"] == 64:
-        feat = (8, 4, 2)
-    else:
-        feat = (mesh.shape["feat"] // 2, 1, 2)
+    feat = {64: (8, 2, 2, 2), 16: (2, 2, 2, 2), 2: (1, 1, 1, 2)}[mesh.shape["feat"]]
     torus = Mesh(
         mesh.devices.reshape(*feat, mesh.shape["row"], mesh.shape["col"]), FEAT + SHARD
     )

time: 99.1 us -> 96.9 us (0.978)
  blocking collectives: 90.3 us -> 88.2 us
    all_to_all x6, blocking collectives: 90.3 us -> 88.2 us  [exchanged(): return lax.all_to_all(x, axis, 0, 0, tiled=True)]
where the time goes in v7:
time: 96.9 us; the launch traced here: 96.6 us
  blocking collectives  88.2 us (91%)
  Pallas kernels  7.65 us (8%)
    all_to_all x6, blocking collectives, exchanged(): return lax.all_to_all(x, axis, 0, 0, tiled=True)  88.2 us
    pallas_call x1, Pallas kernels, local(): call(middle_kernel, held(x.shape), spread_out, scratch_shapes=[pltpu.VMEM...  2.75 us
    pallas_call x1, Pallas kernels, local(): call(first_kernel, spread_out, held((lanes, LOW, rows), jnp.bfloat16), he...  2.32 us

profile of v7, /device:TPU:1, one launch (start us, length us, event | category | flops | bytes accessed | tf_op | source)
XLA Modules:
  0.0 96.6 jit_solution(6497503212916808033)
XLA Ops:
  0.6 2.3 %shard_map.93 = (f32[8,2,16,128]{3,2,1,0:T(8,128)S(1)}, bf16[4,256,512]{2,1,0:T(8,128)(2,1)S(1)}, bf16[4,256,512]{2,1,0:T(8,128)(2,1)S(1)}, f32[8,128]{1,0:T(8,1...) custom-call(f32[8,128]{1,0:T(8,128)S(1)} %broadcast_in_dim.10.place_, ...), custom_call_target="tpu_custom_call" | custom-call | tf_op jit(solution)/shard_map/pallas_call | solution.py:331
  3.0 21.2 %all_to_all.30 = f32[32,8,128]{2,1,0:T(8,128)S(1)} all-to-all(f32[32,8,128]{2,1,0:T(8,128)S(1)} %bitcast.17), channel_id=1, replica_groups=mesh['z'=8,'y_hi'=2,'y_lo'=2,'x_hi'=2,'row'=2,'col'=2] {'z','y_hi','y_lo'}, dimensions={0} | all-to-all | bytes 262144 | tf_op jit(solution)/shard_map/all_to_all | solution.py:307
  24.2 15.2 %all_to_all.31 = f32[32,8,128]{2,1,0:T(8,128)S(1)} all-to-all(f32[32,8,128]{2,1,0:T(8,128)S(1)} %broadcast_in_dim.22), channel_id=1, replica_groups=mesh['z'=8,'y_hi'=2,'y_lo'=2,'x_hi'=2,'row'=2,'col'=2] {'x_hi','z','y_lo'}, dimensions={0} | all-to-all | bytes 262144 | tf_op jit(solution)/shard_map/all_to_all | solution.py:307
  39.4 2.7 %shard_map.94 = (f32[4,256]{1,0:T(4,128)S(1)}, f32[8,2,16,128]{3,2,1,0:T(8,128)S(1)}) custom-call(f32[256,128]{1,0:T(8,128)S(1)} %bitcast.16, bf16[4,256,512]{2,1,0:T(8,128)(2,1)S(1)} %get-tuple-element.26.hot_ref, bf16[4,256,512]{2,1,0:T(8,128)(2,1)S(1)} %get-tuple-element.27.turn_ref, s32[4,512]{1,0:T(4,128)S(1)} %get-tuple-element.28.idx_ref, ...), custom_call_target="tpu_custom_call" | custom-call | tf_op jit(solution)/shard_map/pallas_call | solution.py:348
  42.2 13.6 %all_to_all.32 = f32[32,8,128]{2,1,0:T(8,128)S(1)} all-to-all(f32[32,8,128]{2,1,0:T(8,128)S(1)} %bitcast.18), channel_id=1, replica_groups=mesh['z'=8,'y_hi'=2,'y_lo'=2,'x_hi'=2,'row'=2,'col'=2] {'z','y_hi','y_lo'}, dimensions={0} | all-to-all | bytes 262144 | tf_op jit(solution)/shard_map/all_to_all | solution.py:307
  55.8 13.1 %all_to_all.33 = f32[32,8,128]{2,1,0:T(8,128)S(1)} all-to-all(f32[32,8,128]{2,1,0:T(8,128)S(1)} %broadcast_in_dim.23), channel_id=1, replica_groups=mesh['z'=8,'y_hi'=2,'y_lo'=2,'x_hi'=2,'row'=2,'col'=2] {'x_hi','z','y_lo'}, dimensions={0} | all-to-all | bytes 262144 | tf_op jit(solution)/shard_map/all_to_all | solution.py:307
  68.9 1.8 %shard_map.95 = (f32[4,256]{1,0:T(4,128)S(1)}, f32[8,3,4,256]{3,2,1,0:T(4,128)S(1)}) custom-call(f32[256,128]{1,0:T(8,128)S(1)} %bitcast.15, bf16[4,256,512]{2,1,0:T(8,128)(2,1)S(1)} %get-tuple-element.26.hot_ref, bf16[4,256,512]{2,1,0:T(8,128)(2,1)S(1)} %get-tuple-element.27.turn_ref, s32[4,512]{1,0:T(4,128)S(1)} %get-tuple-element.28.idx_ref, ...), custom_call_target="tpu_custom_call" | custom-call | tf_op jit(solution)/shard_map/pallas_call | solution.py:357
  70.8 12.7 %all_to_all.34.came_ref = f32[8,3,4,256]{3,2,1,0:T(4,128)S(1)} all-to-all(f32[8,3,4,256]{3,2,1,0:T(4,128)S(1)} %get-tuple-element.36), channel_id=1, replica_groups=mesh['z'=8,'y_hi'=2,'y_lo'=2,'x_hi'=2,'row'=2,'col'=2] {'x_hi','row','col'}, dimensions={0} | all-to-all | bytes 196608 | tf_op jit(solution)/shard_map/all_to_all | solution.py:307
  83.5 0.1 shard_map.96
  83.6 12.4 %all_to_all.35 = f32[32,1,128]{2,1,0:T(1,128)S(1)} all-to-all(f32[32,1,128]{2,1,0:T(1,128)S(1)} %bitcast.20), channel_id=1, replica_groups=mesh['z'=8,'y_hi'=2,'y_lo'=2,'x_hi'=2,'row'=2,'col'=2] {'z','y_hi','y_lo'}, dimensions={0} | all-to-all | bytes 32768 | tf_op jit(solution)/shard_map/all_to_all | solution.py:307
  96.0 0.6 shard_map.97
  (5 shorter events, 0.1 us)

commit v8 on v7

--- a/solution.py
+++ b/solution.py
@@ -130,6 +130,18 @@
         for start in range(0, size, LANES)
     ]
     return jnp.concatenate([jnp.concatenate(pieces, axis=0)] * (size // LANES), axis=1)
+
+
+def image_of(hessians, lines):
+    images = [
+        jnp.sum(hessian * as_column(lines[b : b + 1]), axis=0, keepdims=True)
+        for b, hessian in enumerate(hessians)
+    ]
+    return jnp.concatenate(images, axis=0)
+
+
+def sums_of(lines):
+    return jnp.sum(lines, axis=1, keepdims=True)
 
 
 def newton_step(x, target, margins, labels, blk_ref, turn_ref, hot_ref, masks):
@@ -148,24 +160,21 @@
     ]
     hessians = [dot(weighted[b], blk_ref[b], NN) + identity for b in range(blocks)]
     gradient = jnp.concatenate(gradients, axis=0) + penalty * (x - target)
-    delta = jnp.zeros_like(gradient)
-    residual = gradient
-    direction = gradient
-    power = jnp.sum(residual * residual, axis=1, keepdims=True)
-    for cg_step in range(CG_STEPS):
-        image = jnp.concatenate(
-            [
-                jnp.sum(hessians[b] * as_column(direction[b : b + 1]), axis=0, keepdims=True)
-                for b in range(blocks)
-            ],
-            axis=0,
-        )
-        alpha = power / jnp.sum(direction * image, axis=1, keepdims=True)
+    residual = direction = gradient
+    image = image_of(hessians, direction)
+    power = sums_of(residual * residual)
+    alpha = power / sums_of(direction * image)
+    delta = alpha * direction
+    for cg_step in range(1, CG_STEPS):
+        residual = residual - alpha * image
+        turned = image_of(hessians, residual)
+        power_next = sums_of(residual * residual)
+        beta = power_next / power
+        direction = residual + beta * direction
+        image = turned + beta * image
+        power = power_next
+        alpha = power / sums_of(direction * image)
         delta = delta + alpha * direction
-        residual = residual - alpha * image
-        power_next = jnp.sum(residual * residual, axis=1, keepdims=True)
-        direction = residual + (power_next / power) * direction
-        power = power_next
     return x - damping * delta
 
 
@@ -190,18 +199,15 @@
     for copy in (copies[0], copies[1], copies[-1], *blocks, *copies[2:-1]):
         copy.start()
     place_out[...] = place_ref[...]
-    copies[0].wait()
+    for copy in (copies[0], copies[1], copies[-1], *blocks):
+        copy.wait()
     for b in range(blk_ref.shape[0]):
         hot_ref[b] = low_hot(idx_ref[b : b + 1, :])
     masks = masks_of(idx_ref)
-    copies[-1].wait()
     marks = as_table(marks_ref[...].astype(jnp.float32)).astype(jnp.bfloat16)
     found = [dot(marks, hot_ref[b], NN) for b in range(blk_ref.shape[0])]
     label_ref[...] = picked(found, masks)
-    copies[1].wait()
     rounded = x_ref[...].astype(jnp.bfloat16)
-    for copy in blocks:
-        copy.wait()
     partial = []
     for b in range(blk_ref.shape[0]):
         turned = jnp.transpose(blk_ref[b])

time: 96.9 us -> 96.8 us (level)
  no operation moved by 1% of the time
where the time goes in v8:
time: 96.8 us; the launch traced here: 96.5 us
  blocking collectives  88.2 us (91%)
  Pallas kernels  7.51 us (8%)
    all_to_all x6, blocking collectives, exchanged(): return lax.all_to_all(x, axis, 0, 0, tiled=True)  88.2 us
    pallas_call x1, Pallas kernels, local(): call(middle_kernel, held(x.shape), spread_out, scratch_shapes=[pltpu.VMEM...  2.64 us
    pallas_call x1, Pallas kernels, local(): call(first_kernel, spread_out, held((lanes, LOW, rows), jnp.bfloat16), he...  2.4 us

profile of v8, /device:TPU:1, one launch (start us, length us, event | category | flops | bytes accessed | tf_op | source)
XLA Modules:
  0.0 96.5 jit_solution(12673693711811527843)
XLA Ops:
  0.6 2.4 %shard_map.93 = (f32[8,2,16,128]{3,2,1,0:T(8,128)S(1)}, bf16[4,256,512]{2,1,0:T(8,128)(2,1)S(1)}, bf16[4,256,512]{2,1,0:T(8,128)(2,1)S(1)}, f32[8,128]{1,0:T(8,1...) custom-call(f32[8,128]{1,0:T(8,128)S(1)} %broadcast_in_dim.10.place_, ...), custom_call_target="tpu_custom_call" | custom-call | tf_op jit(solution)/shard_map/pallas_call | solution.py:337
  3.0 21.2 %all_to_all.30 = f32[32,8,128]{2,1,0:T(8,128)S(1)} all-to-all(f32[32,8,128]{2,1,0:T(8,128)S(1)} %bitcast.17), channel_id=1, replica_groups=mesh['z'=8,'y_hi'=2,'y_lo'=2,'x_hi'=2,'row'=2,'col'=2] {'z','y_hi','y_lo'}, dimensions={0} | all-to-all | bytes 262144 | tf_op jit(solution)/shard_map/all_to_all | solution.py:313
  24.3 15.2 %all_to_all.31 = f32[32,8,128]{2,1,0:T(8,128)S(1)} all-to-all(f32[32,8,128]{2,1,0:T(8,128)S(1)} %broadcast_in_dim.22), channel_id=1, replica_groups=mesh['z'=8,'y_hi'=2,'y_lo'=2,'x_hi'=2,'row'=2,'col'=2] {'x_hi','z','y_lo'}, dimensions={0} | all-to-all | bytes 262144 | tf_op jit(solution)/shard_map/all_to_all | solution.py:313
  39.5 2.6 %shard_map.94 = (f32[4,256]{1,0:T(4,128)S(1)}, f32[8,2,16,128]{3,2,1,0:T(8,128)S(1)}) custom-call(f32[256,128]{1,0:T(8,128)S(1)} %bitcast.16, bf16[4,256,512]{2,1,0:T(8,128)(2,1)S(1)} %get-tuple-element.26.hot_ref, bf16[4,256,512]{2,1,0:T(8,128)(2,1)S(1)} %get-tuple-element.27.turn_ref, s32[4,512]{1,0:T(4,128)S(1)} %get-tuple-element.28.idx_ref, ...), custom_call_target="tpu_custom_call" | custom-call | tf_op jit(solution)/shard_map/pallas_call | solution.py:354
  42.1 13.6 %all_to_all.32 = f32[32,8,128]{2,1,0:T(8,128)S(1)} all-to-all(f32[32,8,128]{2,1,0:T(8,128)S(1)} %bitcast.18), channel_id=1, replica_groups=mesh['z'=8,'y_hi'=2,'y_lo'=2,'x_hi'=2,'row'=2,'col'=2] {'z','y_hi','y_lo'}, dimensions={0} | all-to-all | bytes 262144 | tf_op jit(solution)/shard_map/all_to_all | solution.py:313
  55.8 13.1 %all_to_all.33 = f32[32,8,128]{2,1,0:T(8,128)S(1)} all-to-all(f32[32,8,128]{2,1,0:T(8,128)S(1)} %broadcast_in_dim.23), channel_id=1, replica_groups=mesh['z'=8,'y_hi'=2,'y_lo'=2,'x_hi'=2,'row'=2,'col'=2] {'x_hi','z','y_lo'}, dimensions={0} | all-to-all | bytes 262144 | tf_op jit(solution)/shard_map/all_to_all | solution.py:313
  68.9 1.7 %shard_map.95 = (f32[4,256]{1,0:T(4,128)S(1)}, f32[8,3,4,256]{3,2,1,0:T(4,128)S(1)}) custom-call(f32[256,128]{1,0:T(8,128)S(1)} %bitcast.15, bf16[4,256,512]{2,1,0:T(8,128)(2,1)S(1)} %get-tuple-element.26.hot_ref, bf16[4,256,512]{2,1,0:T(8,128)(2,1)S(1)} %get-tuple-element.27.turn_ref, s32[4,512]{1,0:T(4,128)S(1)} %get-tuple-element.28.idx_ref, ...), custom_call_target="tpu_custom_call" | custom-call | tf_op jit(solution)/shard_map/pallas_call | solution.py:363
  70.6 12.7 %all_to_all.34.came_ref = f32[8,3,4,256]{3,2,1,0:T(4,128)S(1)} all-to-all(f32[8,3,4,256]{3,2,1,0:T(4,128)S(1)} %get-tuple-element.36), channel_id=1, replica_groups=mesh['z'=8,'y_hi'=2,'y_lo'=2,'x_hi'=2,'row'=2,'col'=2] {'x_hi','row','col'}, dimensions={0} | all-to-all | bytes 196608 | tf_op jit(solution)/shard_map/all_to_all | solution.py:313
  83.4 0.1 shard_map.96
  83.5 12.3 %all_to_all.35 = f32[32,1,128]{2,1,0:T(1,128)S(1)} all-to-all(f32[32,1,128]{2,1,0:T(1,128)S(1)} %bitcast.20), channel_id=1, replica_groups=mesh['z'=8,'y_hi'=2,'y_lo'=2,'x_hi'=2,'row'=2,'col'=2] {'z','y_hi','y_lo'}, dimensions={0} | all-to-all | bytes 32768 | tf_op jit(solution)/shard_map/all_to_all | solution.py:313
  95.8 0.6 shard_map.97
  (5 shorter events, 0.1 us)

commit v9 on v8

--- a/solution.py
+++ b/solution.py
@@ -183,9 +183,7 @@
 
 
 def first_kernel(place_ref, *refs):
-    given, (table_ref, hot_ref, turn_ref, place_out, label_ref, *kept), scratch = refs[:6], refs[6:-3], refs[-3:]
-    marks_ref, sems, block_sems = scratch
-    kept = (*kept, marks_ref)
+    given, (table_ref, hot_ref, turn_ref, place_out, *kept), (sems, block_sems) = refs[:6], refs[6:-2], refs[-2:]
     (idx_in, x_in, blk_in, *_), (idx_ref, x_ref, blk_ref, *_) = given, kept
     copies = [
         pltpu.make_async_copy(src, dst, sems.at[i])
@@ -196,17 +194,16 @@
         pltpu.make_async_copy(blk_in.at[b], blk_ref.at[b], block_sems.at[b])
         for b in range(blk_ref.shape[0])
     ]
-    for copy in (copies[0], copies[1], copies[-1], *blocks, *copies[2:-1]):
+    for copy in (*copies[:2], *blocks, *copies[2:]):
         copy.start()
     place_out[...] = place_ref[...]
-    for copy in (copies[0], copies[1], copies[-1], *blocks):
-        copy.wait()
+    copies[0].wait()
     for b in range(blk_ref.shape[0]):
         hot_ref[b] = low_hot(idx_ref[b : b + 1, :])
     masks = masks_of(idx_ref)
-    marks = as_table(marks_ref[...].astype(jnp.float32)).astype(jnp.bfloat16)
-    found = [dot(marks, hot_ref[b], NN) for b in range(blk_ref.shape[0])]
-    label_ref[...] = picked(found, masks)
+    copies[1].wait()
+    for copy in blocks:
+        copy.wait()
     rounded = x_ref[...].astype(jnp.bfloat16)
     partial = []
     for b in range(blk_ref.shape[0]):
@@ -214,7 +211,7 @@
         turn_ref[b] = turned
         partial.append(dot(rounded, turned, NN)[b : b + 1])
     put(spread(jnp.concatenate(partial, axis=0), hot_ref, masks, NT), table_ref)
-    for copy in copies[2:-1]:
+    for copy in copies[2:]:
         copy.wait()
 
 
@@ -226,8 +223,10 @@
     return total
 
 
-def middle_kernel(margin_ref, hot_ref, turn_ref, idx_ref, x_ref, blk_ref, dual_ref, old_ref, label_ref, x_out, out_ref, stood_ref):
+def middle_kernel(margin_ref, hot_ref, turn_ref, idx_ref, x_ref, blk_ref, dual_ref, old_ref, marks_ref, x_out, out_ref, label_ref, stood_ref):
     masks = masks_of(idx_ref)
+    marks = as_table(marks_ref[...].astype(jnp.float32)).astype(jnp.bfloat16)
+    label_ref[...] = picked([dot(marks, hot_ref[b], NN) for b in range(x_ref.shape[0])], masks)
     for b in range(x_ref.shape[0]):
         stood_ref[b] = jnp.transpose(hot_ref[b])
     target = old_ref[...] - dual_ref[...]
@@ -334,34 +333,33 @@
     zs = lax.axis_size("z")
     spread_out = held((zs, lax.axis_size("y_hi"), marks.shape[0] // zs, LANES))
     given = (index, x, blocks, dual, consensus_old, marks)
-    terms, hots, turned, place, label, index, x, blocks, dual, old = call(
+    terms, hots, turned, place, index, x, blocks, dual, old, marks = call(
         first_kernel,
         spread_out,
         held((lanes, LOW, rows), jnp.bfloat16),
         held((lanes, size, rows), jnp.bfloat16),
         held(place.shape),
-        held(index.shape),
-        *[held(each.shape, each.dtype) for each in given[:-1]],
+        *[held(each.shape, each.dtype) for each in given],
         in_specs=[pl.BlockSpec(memory_space=pltpu.VMEM)] + [HBM] * len(given),
         scratch_shapes=[
-            pltpu.VMEM(marks.shape, marks.dtype),
             pltpu.SemaphoreType.DMA((len(given),)),
             pltpu.SemaphoreType.DMA((lanes,)),
         ],
     )(*in_vmem(place), *in_hbm(*given))
-    kept = (blocks, dual, old, label)
+    kept = (blocks, dual, old)
     margins = tables_to_sum(terms)
-    x, terms = call(
+    x, terms, label = call(
         middle_kernel,
         held(x.shape),
         spread_out,
+        held(index.shape),
         scratch_shapes=[pltpu.VMEM((lanes, rows, LOW), jnp.bfloat16)],
     )(
-        *in_vmem(margins, hots, turned, index, x, *kept)
+        *in_vmem(margins, hots, turned, index, x, *kept, marks)
     )
     margins = tables_to_sum(terms)
     x, sent = call(last_kernel, held(x.shape), held((near, 3, lanes, size)))(
-        *in_vmem(margins, hots, turned, index, x, *kept)
+        *in_vmem(margins, hots, turned, index, x, *kept, label)
     )
     came = exchanged(sent, NEAR)
     consensus, dual, sums = call(

time: 96.8 us -> 96.7 us (level)
  no operation moved by 1% of the time
where the time goes in v9:
time: 96.7 us; the launch traced here: 96.4 us
  blocking collectives  88.2 us (91%)
  Pallas kernels  7.45 us (8%)
    all_to_all x6, blocking collectives, exchanged(): return lax.all_to_all(x, axis, 0, 0, tiled=True)  88.2 us
    pallas_call x1, Pallas kernels, local(): call(middle_kernel, held(x.shape), spread_out, held(index.shape), scratch...  2.82 us
    pallas_call x1, Pallas kernels, local(): call(first_kernel, spread_out, held((lanes, LOW, rows), jnp.bfloat16), he...  2.17 us

profile of v9, /device:TPU:1, one launch (start us, length us, event | category | flops | bytes accessed | tf_op | source)
XLA Modules:
  0.0 96.4 jit_solution(5201795015858515353)
XLA Ops:
  0.6 2.2 %shard_map.93 = (f32[8,2,16,128]{3,2,1,0:T(8,128)S(1)}, bf16[4,256,512]{2,1,0:T(8,128)(2,1)S(1)}, bf16[4,256,512]{2,1,0:T(8,128)(2,1)S(1)}, f32[8,128]{1,0:T(8,1...) custom-call(f32[8,128]{1,0:T(8,128)S(1)} %broadcast_in_dim.10.place_, ...), custom_call_target="tpu_custom_call" | custom-call | tf_op jit(solution)/shard_map/pallas_call | solution.py:336
  2.8 21.2 %all_to_all.30 = f32[32,8,128]{2,1,0:T(8,128)S(1)} all-to-all(f32[32,8,128]{2,1,0:T(8,128)S(1)} %bitcast.17), channel_id=1, replica_groups=mesh['z'=8,'y_hi'=2,'y_lo'=2,'x_hi'=2,'row'=2,'col'=2] {'z','y_hi','y_lo'}, dimensions={0} | all-to-all | bytes 262144 | tf_op jit(solution)/shard_map/all_to_all | solution.py:312
  24.0 15.2 %all_to_all.31 = f32[32,8,128]{2,1,0:T(8,128)S(1)} all-to-all(f32[32,8,128]{2,1,0:T(8,128)S(1)} %broadcast_in_dim.22), channel_id=1, replica_groups=mesh['z'=8,'y_hi'=2,'y_lo'=2,'x_hi'=2,'row'=2,'col'=2] {'x_hi','z','y_lo'}, dimensions={0} | all-to-all | bytes 262144 | tf_op jit(solution)/shard_map/all_to_all | solution.py:312
  39.3 2.8 %shard_map.94 = (f32[4,256]{1,0:T(4,128)S(1)}, f32[8,2,16,128]{3,2,1,0:T(8,128)S(1)}, f32[4,512]{1,0:T(4,128)S(1)}) custom-call(f32[256,128]{1,0:T(8,128)S(1)} %bitcast.16, bf16[4,256,512]{2,1,0:T(8,128)(2,1)S(1)} %get-tuple-element.27.hot_ref, bf16[4,256,512]{2,1,0:T(8,128)(2,1)S(1)} %get-tuple-element.28.turn_ref, s32[4,512]{1,0:T(4,128)S(1)} %get-tuple-element.29.idx_ref, ...), custom_call_target="tpu_custom_call" | custom-call | tf_op jit(solution)/shard_map/pallas_call | solution.py:351
  42.1 13.6 %all_to_all.32 = f32[32,8,128]{2,1,0:T(8,128)S(1)} all-to-all(f32[32,8,128]{2,1,0:T(8,128)S(1)} %bitcast.18), channel_id=1, replica_groups=mesh['z'=8,'y_hi'=2,'y_lo'=2,'x_hi'=2,'row'=2,'col'=2] {'z','y_hi','y_lo'}, dimensions={0} | all-to-all | bytes 262144 | tf_op jit(solution)/shard_map/all_to_all | solution.py:312
  55.7 13.1 %all_to_all.33 = f32[32,8,128]{2,1,0:T(8,128)S(1)} all-to-all(f32[32,8,128]{2,1,0:T(8,128)S(1)} %broadcast_in_dim.23), channel_id=1, replica_groups=mesh['z'=8,'y_hi'=2,'y_lo'=2,'x_hi'=2,'row'=2,'col'=2] {'x_hi','z','y_lo'}, dimensions={0} | all-to-all | bytes 262144 | tf_op jit(solution)/shard_map/all_to_all | solution.py:312
  68.9 1.7 %shard_map.95 = (f32[4,256]{1,0:T(4,128)S(1)}, f32[8,3,4,256]{3,2,1,0:T(4,128)S(1)}) custom-call(f32[256,128]{1,0:T(8,128)S(1)} %bitcast.15, bf16[4,256,512]{2,1,0:T(8,128)(2,1)S(1)} %get-tuple-element.27.hot_ref, bf16[4,256,512]{2,1,0:T(8,128)(2,1)S(1)} %get-tuple-element.28.turn_ref, s32[4,512]{1,0:T(4,128)S(1)} %get-tuple-element.29.idx_ref, ...), custom_call_target="tpu_custom_call" | custom-call | tf_op jit(solution)/shard_map/pallas_call | solution.py:361
  70.6 12.8 %all_to_all.34.came_ref = f32[8,3,4,256]{3,2,1,0:T(4,128)S(1)} all-to-all(f32[8,3,4,256]{3,2,1,0:T(4,128)S(1)} %get-tuple-element.38), channel_id=1, replica_groups=mesh['z'=8,'y_hi'=2,'y_lo'=2,'x_hi'=2,'row'=2,'col'=2] {'x_hi','row','col'}, dimensions={0} | all-to-all | bytes 196608 | tf_op jit(solution)/shard_map/all_to_all | solution.py:312
  83.3 0.1 shard_map.96
  83.4 12.3 %all_to_all.35 = f32[32,1,128]{2,1,0:T(1,128)S(1)} all-to-all(f32[32,1,128]{2,1,0:T(1,128)S(1)} %bitcast.20), channel_id=1, replica_groups=mesh['z'=8,'y_hi'=2,'y_lo'=2,'x_hi'=2,'row'=2,'col'=2] {'z','y_hi','y_lo'}, dimensions={0} | all-to-all | bytes 32768 | tf_op jit(solution)/shard_map/all_to_all | solution.py:312
  95.8 0.6 shard_map.97
  (5 shorter events, 0.1 us)

commit v10 on v9

--- a/solution.py
+++ b/solution.py
@@ -144,11 +144,17 @@
     return jnp.sum(lines, axis=1, keepdims=True)
 
 
-def newton_step(x, target, margins, labels, blk_ref, turn_ref, hot_ref, masks):
+def newton_step(x, target, margins, label_ref, blk_ref, turn_ref, hot_ref, masks, marks_ref=None):
     blocks, size = x.shape
-    tables = jnp.concatenate(three_parts(as_table(margins)), axis=0).astype(jnp.bfloat16)
+    tables = three_parts(as_table(margins))
+    if marks_ref is not None:
+        tables += (as_table(marks_ref[...].astype(jnp.float32)),)
+    tables = jnp.concatenate(tables, axis=0).astype(jnp.bfloat16)
     found = [dot(tables, hot_ref[b], NN) for b in range(blocks)]
-    found = [each[:HIGH] + each[HIGH : 2 * HIGH] + each[2 * HIGH :] for each in found]
+    if marks_ref is not None:
+        label_ref[...] = picked([each[3 * HIGH :] for each in found], masks)
+    labels = label_ref[...]
+    found = [each[:HIGH] + each[HIGH : 2 * HIGH] + each[2 * HIGH : 3 * HIGH] for each in found]
     prob = 1.0 / (1.0 + jnp.exp(-picked(found, masks)))
     misfit = (prob - labels).astype(jnp.bfloat16)
     weight = prob * (1.0 - prob)
@@ -225,13 +231,11 @@
 
 def middle_kernel(margin_ref, hot_ref, turn_ref, idx_ref, x_ref, blk_ref, dual_ref, old_ref, marks_ref, x_out, out_ref, label_ref, stood_ref):
     masks = masks_of(idx_ref)
-    marks = as_table(marks_ref[...].astype(jnp.float32)).astype(jnp.bfloat16)
-    label_ref[...] = picked([dot(marks, hot_ref[b], NN) for b in range(x_ref.shape[0])], masks)
     for b in range(x_ref.shape[0]):
         stood_ref[b] = jnp.transpose(hot_ref[b])
     target = old_ref[...] - dual_ref[...]
     x = newton_step(
-        x_ref[...], target, summed(margin_ref), label_ref[...], blk_ref, turn_ref, hot_ref, masks
+        x_ref[...], target, summed(margin_ref), label_ref, blk_ref, turn_ref, hot_ref, masks, marks_ref
     )
     x_out[...] = x
     rounded = x.astype(jnp.bfloat16)
@@ -246,7 +250,7 @@
     dual = dual_ref[...]
     old = old_ref[...]
     x = newton_step(
-        x_ref[...], old - dual, summed(margin_ref), label_ref[...], blk_ref, turn_ref, hot_ref, masks
+        x_ref[...], old - dual, summed(margin_ref), label_ref, blk_ref, turn_ref, hot_ref, masks
     )
     x_out[...] = x
     for peer in range(sent_ref.shape[0]):

time: 96.7 us -> 96.6 us (level)
  no operation moved by 1% of the time
where the time goes in v10:
time: 96.6 us; the launch traced here: 96.3 us
  blocking collectives  88.2 us (91%)
  Pallas kernels  7.29 us (8%)
    all_to_all x6, blocking collectives, exchanged(): return lax.all_to_all(x, axis, 0, 0, tiled=True)  88.2 us
    pallas_call x1, Pallas kernels, local(): call(middle_kernel, held(x.shape), spread_out, held(index.shape), scratch...  2.65 us
    pallas_call x1, Pallas kernels, local(): call(first_kernel, spread_out, held((lanes, LOW, rows), jnp.bfloat16), he...  2.17 us

profile of v10, /device:TPU:1, one launch (start us, length us, event | category | flops | bytes accessed | tf_op | source)
XLA Modules:
  0.0 96.3 jit_solution(3019104663941412136)
XLA Ops:
  0.6 2.2 %shard_map.93 = (f32[8,2,16,128]{3,2,1,0:T(8,128)S(1)}, bf16[4,256,512]{2,1,0:T(8,128)(2,1)S(1)}, bf16[4,256,512]{2,1,0:T(8,128)(2,1)S(1)}, f32[8,128]{1,0:T(8,1...) custom-call(f32[8,128]{1,0:T(8,128)S(1)} %broadcast_in_dim.10.place_, ...), custom_call_target="tpu_custom_call" | custom-call | tf_op jit(solution)/shard_map/pallas_call | solution.py:340
  2.8 21.2 %all_to_all.30 = f32[32,8,128]{2,1,0:T(8,128)S(1)} all-to-all(f32[32,8,128]{2,1,0:T(8,128)S(1)} %bitcast.17), channel_id=1, replica_groups=mesh['z'=8,'y_hi'=2,'y_lo'=2,'x_hi'=2,'row'=2,'col'=2] {'z','y_hi','y_lo'}, dimensions={0} | all-to-all | bytes 262144 | tf_op jit(solution)/shard_map/all_to_all | solution.py:316
  24.0 15.2 %all_to_all.31 = f32[32,8,128]{2,1,0:T(8,128)S(1)} all-to-all(f32[32,8,128]{2,1,0:T(8,128)S(1)} %broadcast_in_dim.22), channel_id=1, replica_groups=mesh['z'=8,'y_hi'=2,'y_lo'=2,'x_hi'=2,'row'=2,'col'=2] {'x_hi','z','y_lo'}, dimensions={0} | all-to-all | bytes 262144 | tf_op jit(solution)/shard_map/all_to_all | solution.py:316
  39.3 2.7 %shard_map.94 = (f32[4,256]{1,0:T(4,128)S(1)}, f32[8,2,16,128]{3,2,1,0:T(8,128)S(1)}, f32[4,512]{1,0:T(4,128)S(1)}) custom-call(f32[256,128]{1,0:T(8,128)S(1)} %bitcast.16, bf16[4,256,512]{2,1,0:T(8,128)(2,1)S(1)} %get-tuple-element.27.hot_ref, bf16[4,256,512]{2,1,0:T(8,128)(2,1)S(1)} %get-tuple-element.28.turn_ref, s32[4,512]{1,0:T(4,128)S(1)} %get-tuple-element.29.idx_ref, ...), custom_call_target="tpu_custom_call" | custom-call | tf_op jit(solution)/shard_map/pallas_call | solution.py:355
  41.9 13.6 %all_to_all.32 = f32[32,8,128]{2,1,0:T(8,128)S(1)} all-to-all(f32[32,8,128]{2,1,0:T(8,128)S(1)} %bitcast.18), channel_id=1, replica_groups=mesh['z'=8,'y_hi'=2,'y_lo'=2,'x_hi'=2,'row'=2,'col'=2] {'z','y_hi','y_lo'}, dimensions={0} | all-to-all | bytes 262144 | tf_op jit(solution)/shard_map/all_to_all | solution.py:316
  55.6 13.1 %all_to_all.33 = f32[32,8,128]{2,1,0:T(8,128)S(1)} all-to-all(f32[32,8,128]{2,1,0:T(8,128)S(1)} %broadcast_in_dim.23), channel_id=1, replica_groups=mesh['z'=8,'y_hi'=2,'y_lo'=2,'x_hi'=2,'row'=2,'col'=2] {'x_hi','z','y_lo'}, dimensions={0} | all-to-all | bytes 262144 | tf_op jit(solution)/shard_map/all_to_all | solution.py:316
  68.7 1.7 %shard_map.95 = (f32[4,256]{1,0:T(4,128)S(1)}, f32[8,3,4,256]{3,2,1,0:T(4,128)S(1)}) custom-call(f32[256,128]{1,0:T(8,128)S(1)} %bitcast.15, bf16[4,256,512]{2,1,0:T(8,128)(2,1)S(1)} %get-tuple-element.27.hot_ref, bf16[4,256,512]{2,1,0:T(8,128)(2,1)S(1)} %get-tuple-element.28.turn_ref, s32[4,512]{1,0:T(4,128)S(1)} %get-tuple-element.29.idx_ref, ...), custom_call_target="tpu_custom_call" | custom-call | tf_op jit(solution)/shard_map/pallas_call | solution.py:365
  70.4 12.8 %all_to_all.34.came_ref = f32[8,3,4,256]{3,2,1,0:T(4,128)S(1)} all-to-all(f32[8,3,4,256]{3,2,1,0:T(4,128)S(1)} %get-tuple-element.38), channel_id=1, replica_groups=mesh['z'=8,'y_hi'=2,'y_lo'=2,'x_hi'=2,'row'=2,'col'=2] {'x_hi','row','col'}, dimensions={0} | all-to-all | bytes 196608 | tf_op jit(solution)/shard_map/all_to_all | solution.py:316
  83.2 0.1 shard_map.96
  83.3 12.3 %all_to_all.35 = f32[32,1,128]{2,1,0:T(1,128)S(1)} all-to-all(f32[32,1,128]{2,1,0:T(1,128)S(1)} %bitcast.20), channel_id=1, replica_groups=mesh['z'=8,'y_hi'=2,'y_lo'=2,'x_hi'=2,'row'=2,'col'=2] {'z','y_hi','y_lo'}, dimensions={0} | all-to-all | bytes 32768 | tf_op jit(solution)/shard_map/all_to_all | solution.py:316
  95.6 0.6 shard_map.97
  (5 shorter events, 0.1 us)
